TPU v7x, 32 devices: a whole 2x2x4 slice. The times are simulated.
32 devices in a mesh: dp: 8 (over z, y), rows: 4 (over x, core).
Axes of the slice: x: 2, y: 2, z: 4, core: 2. Of those that a mesh axis runs over, the one named last changes fastest.
Arguments:
- real_frames: bfloat16 [8, 3, 64, 256], P('dp', None, 'rows'), may hold values from -4 to 4
- fake_frames: bfloat16 [8, 3, 64, 256], P('dp', None, 'rows'), may hold values from -4 to 4
- conv_one: bfloat16 [3, 3, 3, 64], replicated, may hold values from -1.25 to 1.25
- conv_two: bfloat16 [3, 3, 64, 128], replicated, may hold values from -0.25 to 0.25
- conv_three: bfloat16 [3, 3, 128, 256], replicated, may hold values from -0.1875 to 0.1875
- conv_four: bfloat16 [3, 3, 256, 512], replicated, may hold values from -0.125 to 0.125
- conv_five: bfloat16 [3, 3, 512, 512], replicated, may hold values from -0.09375 to 0.09375
- bias_one: float32 [64], replicated, may hold values from -2 to 2
- bias_two: float32 [128], replicated, may hold values from -2 to 2
- bias_three: float32 [256], replicated, may hold values from -2 to 2
- bias_four: float32 [512], replicated, may hold values from -2 to 2
- bias_five: float32 [512], replicated, may hold values from -2 to 2
- linear_one: float32 [64], replicated, may hold values from 0.05 to 2
- linear_two: float32 [128], replicated, may hold values from 0.05 to 2
- linear_three: float32 [256], replicated, may hold values from 0.05 to 2
- linear_four: float32 [512], replicated, may hold values from 0.05 to 2
- linear_five: float32 [512], replicated, may hold values from 0.25 to 10
Outputs:
- tap_losses: float32 [5], replicated
- fake_grad: float32 [8, 3, 64, 256], P('dp', None, 'rows')
All inputs are finite; a program needn't handle non-finite values.
Results may differ from a plain program's by a relative error of at most 0.0065.
Values may be sent and summed in bfloat16 or wider, within the bound.
No kernel may reach another device: no remote copies, remote signals or barrier semaphores. Data moves between devices by JAX's collectives and lax.ppermute only.
A program may use at most 128 MiB of HBM per device.

v0:
```python
import functools
import math

import jax
import jax.numpy as jnp
from jax import lax
from jax.experimental import pallas as pl
from jax.experimental.pallas import tpu as pltpu
from jax.sharding import PartitionSpec as P

EPS = 1e-06
F32 = jnp.float32
BF16 = jnp.bfloat16
K0 = math.sqrt(2.0 / math.pi)
K1 = K0 * 0.044715
PH = 16
LANES = 128
HALF = 64
ONE = (PH + 2) * 3
MIB = 1 << 20
VM = pl.BlockSpec(memory_space=pltpu.VMEM)
HBM = pl.BlockSpec(memory_space=pltpu.HBM)


def gelu(h):
    t = jnp.tanh(h * (2.0 * K0 + (8.0 * K1) * (h * h)))
    return h + h * t


def gelu_back(h):
    sq = h * h
    t = jnp.tanh(h * (2.0 * K0 + (8.0 * K1) * sq))
    return (0.5 + 0.5 * t) + (h * (1.0 - t * t)) * (K0 + (12.0 * K1) * sq)


def dot(a, b):
    return lax.dot_general(a, b, (((1,), (0,)), ((), ())), preferred_element_type=F32)


def dot_t(a, b):
    return lax.dot_general(a, b, (((1,), (1,)), ((), ())), preferred_element_type=F32)


def iota(shape, dim):
    return lax.broadcasted_iota(jnp.int32, shape, dim)


def low_half(shape):
    return iota(shape, len(shape) - 1) % LANES < HALF


def shifted(value, step):
    n, length, chans = value.shape
    flat = value.reshape(n * length, chans)
    place = iota(flat.shape, 0) % length
    if step > 0:
        out = jnp.where(place == 0, 0.0, pltpu.roll(flat, 1, 0))
    else:
        out = jnp.where(place == length - 1, 0.0, pltpu.roll(flat, n * length - 1, 0))
    return out.reshape(n, length, chans)


def call(body, outs, ins, name, scratch=(), limit=16, flops=0, far=()):
    far = [pltpu.with_memory_space_constraint(v, pltpu.HBM) for v in far]
    return pl.pallas_call(
        body,
        out_shape=outs,
        in_specs=[HBM] * len(far) + [VM] * len(ins),
        out_specs=jax.tree.map(lambda _: VM, outs),
        scratch_shapes=scratch,
        name=name,
        cost_estimate=pl.CostEstimate(flops=flops, transcendentals=0, bytes_accessed=0),
        compiler_params=pltpu.CompilerParams(vmem_limit_bytes=limit * MIB),
    )(*far, *ins)


def prep_body(
    real_hbm, fake_hbm, c1_hbm, c2_hbm, b1_hbm,
    out_ref, c1, c2, b1, real_ref, fake_ref, sems,
):
    pairs = ((real_hbm, real_ref), (fake_hbm, fake_ref), (c1_hbm, c1), (c2_hbm, c2), (b1_hbm, b1))
    copies = [pltpu.make_async_copy(a, b, sems.at[i]) for i, (a, b) in enumerate(pairs)]
    for copy in copies:
        copy.start()
    _, rows, width = real_ref.shape
    length = width // PH
    shape = (rows * length, width)
    col = iota(shape, 1)
    place = iota(shape, 0) % length
    inside = col // PH == place
    edges = (col == place * PH - 1) | (col == place * PH + PH)
    eshape = (width, LANES)
    ecol = iota(eshape, 0) % PH
    lane = iota(eshape, 1)
    total = jnp.zeros((rows * length, LANES), F32)
    for copy in copies:
        copy.wait()
    for img, ref in enumerate((real_ref, fake_ref)):
        for ch in range(3):
            x = ref[ch].astype(F32)
            wide = jnp.broadcast_to(x[:, None, :], (rows, length, width)).reshape(shape)
            base = img * HALF + ch
            a = jnp.concatenate(
                [jnp.where(inside, wide, 0.0), jnp.where(edges, wide, 0.0)], axis=1
            ).astype(BF16)
            e_in = lane == base + (ecol + 1) * 3
            e_edge = ((ecol == PH - 1) & (lane == base)) | (
                (ecol == 0) & (lane == base + (PH + 1) * 3)
            )
            e = jnp.concatenate(
                [jnp.where(e_in, 1.0, 0.0), jnp.where(e_edge, 1.0, 0.0)], axis=0
            ).astype(BF16)
            total = total + dot(a, e)
    lane = iota(total.shape, 1) % HALF
    total = jnp.where((lane >= ONE) & (lane < ONE + 3), 1.0, total)
    out_ref[...] = total.astype(BF16).reshape(rows, length, LANES)


def prep(real, fake, c1, c2, b1):
    _, rows, width = real.shape
    V = pltpu.VMEM
    return call(
        prep_body,
        (V((rows, width // PH, LANES), BF16), V(c1.shape, BF16), V(c2.shape, BF16), V(b1.shape, F32)),
        (),
        "prep",
        (V(real.shape, BF16), V(fake.shape, BF16), pltpu.SemaphoreType.DMA((5,))),
        limit=8,
        far=(real, fake, c1, c2, b1),
    )


def weights_body(c1_ref, c2_ref, b1_ref, w1, r1, w2, w2t, base, bias):
    C1, C2 = c2_ref.shape[1:]
    base[...] = jnp.zeros(base.shape, F32)
    for dr in range(3):
        for dc in range(3):
            blk = c1_ref[dr, dc].astype(F32)
            base[dr, dc * 3 : dc * 3 + 3, 0:HALF] = blk
            base[dr, dc * 3 : dc * 3 + 3, HALF:LANES] = blk
    bias[0:1, 0:HALF] = b1_ref[...]
    bias[0:1, HALF:LANES] = b1_ref[...]
    left = bias[0:1, :]
    shape = (HALF, LANES)
    row = iota(shape, 0)
    lo = low_half(shape)
    extra = jnp.zeros(shape, F32)
    for k in range(3):
        part = left.astype(BF16).astype(F32)
        extra = jnp.where(row == ONE + k, jnp.broadcast_to(part, shape), extra)
        left = left - part
    for dr in range(3):
        b = base[dr]
        for i in range(PH // 2):
            first = pltpu.roll(b, (6 * i) % HALF, 0) if i else b
            blk = jnp.where(lo, first, pltpu.roll(b, (6 * i + 3) % HALF, 0))
            if dr == 1:
                blk = blk + extra
            w1[dr * HALF : (dr + 1) * HALF, i * LANES : (i + 1) * LANES] = (0.5 * blk).astype(BF16)
        b = base[2 - dr]
        for j in range(PH // 2 + 2):
            s0, s1 = ((6 * j - 9) % HALF, (6 * j - 6) % HALF)
            blk = jnp.where(
                lo, pltpu.roll(b, s0, 0) if s0 else b, pltpu.roll(b, s1, 0) if s1 else b
            )
            k = (dr * (PH // 2 + 2) + j) * LANES
            r1[:, k : k + LANES] = blk.astype(BF16)
    w1[3 * HALF : 4 * HALF, :] = jnp.zeros((HALF, w1.shape[1]), BF16)
    w2[...] = jnp.zeros(w2.shape, BF16)
    w2t[...] = jnp.zeros(w2t.shape, BF16)
    slot = (2, 0, 1, 3)
    for dr in range(3):
        for dc in range(3):
            blk = c2_ref[dr * 3 + dc]
            back = c2_ref[(2 - dr) * 3 + 2 - dc]
            for u in range(2):
                k = (dr * 4 + slot[dc + u]) * C1
                w2[k : k + C1, u * C2 : (u + 1) * C2] = blk
                k = (dr * 4 + dc + u) * C2
                for d in range(2):
                    n = (u * 2 + d) * C1
                    w2t[n : n + C1, k : k + C2] = back


def three(load):
    return jnp.concatenate([load(dr, dc) for dr in range(3) for dc in range(3)], axis=1)


def pooled_into(ref, img, row, value):
    rows, phases = value.shape[0:2]
    at = pl.ds(row + 1, rows)
    ref[img, at, 1 : phases + 1] = value.astype(BF16)
    ref[img, at, 0] = shifted(value[:, phases - 1], 1).astype(BF16)
    ref[img, at, phases + 1] = shifted(value[:, 0], -1).astype(BF16)


def inverse_norms(r, f, ones2, chans):
    sums = dot(jnp.concatenate([r * r, f * f], axis=1).astype(BF16), ones2)
    reps = chans // LANES

    def spread(v):
        return jnp.concatenate([v] * reps, axis=1) if reps > 1 else v

    inv = lax.rsqrt(sums + EPS)
    return spread(inv[:, 0:LANES]), spread(inv[:, LANES : 2 * LANES])


def ones_for(seg, chans):
    rr = iota((2 * chans, 2 * LANES), 0)
    cc = iota((2 * chans, 2 * LANES), 1)
    if seg == 1:
        return jnp.where(rr // HALF == cc // HALF, 1.0, 0.0).astype(BF16)
    return jnp.where(rr // chans == cc // LANES, 1.0, 0.0).astype(BF16)


def forward_body(
    dims,
    *refs,
):
    far, refs = (refs[0:12], refs[12:])
    x_ref, w1, w2, loss_ref, a1, a2, a3, a4, a5, z1, z2, z3, z4, z5 = refs[0:14]
    near, refs = (refs[14:26], refs[26:])
    w3, w4, w5, b2_ref, b3_ref, b4_ref, b5_ref, l1_ref, l2_ref, l3_ref, l4_ref, l5_ref = near
    xk, p1, p2, p3, p4, sems = refs
    copies = [pltpu.make_async_copy(a, b, sems.at[i]) for i, (a, b) in enumerate(zip(far, near))]
    for copy in copies[3:] + copies[:3]:
        copy.start()
    H, L, HB, C1, C2, C3, C4, C5 = dims
    ph2, ph3, ph4 = (PH // 2, PH // 4, PH // 8)
    band = lax.axis_index("rows")
    for p in (p1, p2, p3, p4):
        n = p.shape[1]
        for img in range(2):
            p[img, 0] = jnp.zeros(p.shape[2:], BF16)
            p[img, n - 1] = jnp.zeros(p.shape[2:], BF16)

    x = x_ref[...].astype(F32)
    xr = pltpu.roll(x.reshape(H * L, LANES), HALF, 1).reshape(H, L, LANES)
    zero = jnp.zeros((1, L, LANES), F32)
    lo3 = low_half((H, L, LANES))

    def above(v):
        return jnp.concatenate([zero, v[: H - 1]], axis=0)

    def below(v):
        return jnp.concatenate([v[1:], zero], axis=0)

    xk[0, :, :, 0:LANES] = jnp.where(lo3, above(x), xr).astype(BF16)
    xk[0, :, :, LANES : 2 * LANES] = below(x).astype(BF16)
    xk[1, :, :, 0:LANES] = jnp.where(lo3, above(xr), x).astype(BF16)
    xk[1, :, :, LANES : 2 * LANES] = below(xr).astype(BF16)

    def keep(r0, rows, size, first):
        place = r0 - first
        return pl.ds(jnp.where((place >= 0) & (place < size), place, size), rows)

    rows = ROWS1

    @pl.loop(0, H // rows)
    def _(step):
        r0 = step * rows
        kept = keep(r0, rows, HB + 2 * rows, band * HB - rows)
        at = pl.ds(r0 // 2 + 1, rows // 2)
        for img in range(2):
            lhs = xk[img, pl.ds(r0, rows)].reshape(rows * L, 2 * LANES)
            for n in range(PH // 4):
                h = dot(lhs, w1[:, n * 256 : (n + 1) * 256])
                act = gelu(h)
                for i in range(2):
                    lanes = slice(i * LANES, (i + 1) * LANES)
                    part = act[:, lanes].reshape(rows, L, LANES)
                    a1[img, kept, n * 2 + i] = part.astype(BF16)
                    if img:
                        z1[kept, n * 2 + i] = h[:, lanes].reshape(rows, L, LANES)
                    pair = part.reshape(rows // 2, 2, L, LANES)
                    s = (pair[:, 0] + pair[:, 1]).reshape(rows // 2 * L, LANES)
                    s = ((s + pltpu.roll(s, HALF, 1)) * 0.125).reshape(rows // 2, L, LANES)
                    half = slice(i * HALF, (i + 1) * HALF)
                    p1[img, at, n, :, half] = s.astype(BF16)[..., half]
                    q = n * 2 + i
                    other = slice((1 - i) * HALF, (2 - i) * HALF)
                    if q == ph2 - 1:
                        s = shifted(s, 1)
                    if q == 0:
                        s = shifted(s, -1)
                    slot = ph3 + (n + 1 if i else n - 1) % ph3
                    p1[img, at, slot, :, other] = s.astype(BF16)[..., other]

    for copy in copies[3:]:
        copy.wait()

    rows2 = ROWS2
    bias = jnp.concatenate([b2_ref[...]] * 2, axis=1) * 0.5

    @pl.loop(0, H // 2 // rows2)
    def _(step):
        r0 = step * rows2
        kept = keep(r0, rows2, HB // 2 + 2 * rows2, band * (HB // 2) - rows2)
        for img in range(2):
            lhs = jnp.concatenate(
                [
                    p1[img, pl.ds(r0 + dr, rows2), k * ph3 : (k + 1) * ph3].reshape(
                        rows2 * ph3 * L, LANES
                    )
                    for dr in range(3)
                    for k in range(2)
                ],
                axis=1,
            )
            h = dot(lhs, w2[...]) + bias
            act = gelu(h)
            for u in range(2):
                lanes = slice(u * C2, (u + 1) * C2)
                a2[img, kept, u] = act[:, lanes].astype(BF16).reshape(rows2, ph3, L, C2)
                if img:
                    z2[kept, u] = h[:, lanes].reshape(rows2, ph3, L, C2)
            s = (act[:, 0:C2] + act[:, C2 : 2 * C2]).reshape(rows2 // 2, 2, ph3, L, C2)
            pooled_into(p2, img, r0 // 2, (s[:, 0] + s[:, 1]) * 0.125)

    copies[0].wait()
    rows3 = ROWS3
    bias3 = b3_ref[...] * 0.5

    @pl.loop(0, H // 4 // rows3)
    def _(step):
        r0 = step * rows3
        kept = keep(r0, rows3, HB // 4 + 2 * rows3, band * (HB // 4) - rows3)
        for img in range(2):
            lhs = three(
                lambda dr, dc: p2[img, pl.ds(r0 + dr, rows3), dc : dc + ph3].reshape(
                    rows3 * ph3 * L, C2
                )
            )
            h = dot(lhs, w3[...]) + bias3
            act = gelu(h)
            a3[img, kept] = act.astype(BF16).reshape(rows3, ph3, L, C3)
            if img:
                z3[kept] = h.reshape(rows3, ph3, L, C3)
            pair = act.reshape(rows3 // 2, 2, ph4, 2, L, C3)
            pooled = (pair[:, 0, :, 0] + pair[:, 0, :, 1]) + (pair[:, 1, :, 0] + pair[:, 1, :, 1])
            pooled_into(p3, img, r0 // 2, pooled * 0.125)

    copies[1].wait()
    rows4 = ROWS4
    bias4 = b4_ref[...] * 0.5

    @pl.loop(0, H // 8 // rows4)
    def _(step):
        r0 = step * rows4
        for img in range(2):
            lhs = three(
                lambda dr, dc: p3[img, pl.ds(r0 + dr, rows4), dc : dc + ph4].reshape(
                    rows4 * ph4 * L, C3
                )
            )
            h = dot(lhs, w4[...]) + bias4
            act = gelu(h)
            at = pl.ds(r0 + 2, rows4)
            a4[img, at] = act.astype(BF16).reshape(rows4, ph4, L, C4)
            if img:
                z4[at] = h.reshape(rows4, ph4, L, C4)
            pair = act.reshape(rows4 // 2, 2, ph4, L, C4)
            pooled = (pair[:, 0, 0] + pair[:, 0, 1]) + (pair[:, 1, 0] + pair[:, 1, 1])
            pooled_into(p4, img, r0 // 2, (pooled * 0.125)[:, None])

    copies[2].wait()
    h5 = H // 16
    lhs = jnp.concatenate(
        [
            three(lambda dr, dc: p4[img, dr : dr + h5, dc].reshape(h5 * L, C4))
            for img in range(2)
        ],
        axis=0,
    )
    h = dot(lhs, w5[...]) + b5_ref[...] * 0.5
    act = gelu(h).astype(BF16)
    for img in range(2):
        a5[img, 2 : 2 + h5, 0] = act[img * h5 * L : (img + 1) * h5 * L].reshape(h5, L, C5)
    z5[2 : 2 + h5, 0] = h[h5 * L :].reshape(h5, L, C5)

    loss_ref[...] = jnp.zeros(loss_ref.shape, F32)
    places = (rows, rows2, rows3, 2 + band * (HB // 8), 2 + band * (HB // 16))
    chunks = (4, 4, 4, 2, 1)
    for s, (acts, l_ref) in enumerate(
        ((a1, l1_ref), (a2, l2_ref), (a3, l3_ref), (a4, l4_ref), (a5, l5_ref))
    ):
        chans = acts.shape[-1]
        ones2 = ones_for(s + 1, chans)
        own, chunk = (HB >> s, chunks[s])
        m = chunk * math.prod(acts.shape[2:-1])
        lin = l_ref[...]
        if s == 0:
            lin = jnp.concatenate([lin, lin], axis=1)

        def piece(k, s=s, acts=acts, ones2=ones2, chunk=chunk, m=m, chans=chans, lin=lin):
            at = pl.ds(places[s] + k * chunk, chunk)
            r = acts[0, at].reshape(m, chans).astype(F32)
            f = acts[1, at].reshape(m, chans).astype(F32)
            inv_r, inv_f = inverse_norms(r, f, ones2, chans)
            d = r * inv_r - f * inv_f
            part = jnp.sum(d * d, axis=0, keepdims=True) * lin
            acc = part[:, 0:LANES]
            for j in range(1, chans // LANES):
                acc = acc + part[:, j * LANES : (j + 1) * LANES]
            loss_ref[s : s + 1, :] += acc

        if own == chunk:
            piece(0)
        else:
            pl.loop(0, own // chunk)(piece)


def taps(seg, acts, pres, grads, l_ref, band, HB, H, up, local, halo, chunk):
    chans = acts.shape[-1]
    inner = acts.shape[2:-1]
    m = chunk * math.prod(inner)
    L = inner[-1]
    own = HB >> (seg - 1)
    total_rows = H >> (seg - 1)
    start = band * own - halo
    scale = -2.0 * 4.0 ** (seg - 1)
    ones2 = ones_for(seg, chans)
    ones1 = ones2[0:LANES, 0:LANES] if seg == 1 else jnp.ones((chans, LANES), BF16)
    reps = chans // LANES
    lin = l_ref[...]
    if seg == 1:
        lin = jnp.concatenate([lin, lin], axis=1)

    def piece(k):
        i0 = k * chunk
        at = pl.ds(local + i0, chunk)
        r = acts[0, at].reshape(m, chans).astype(F32)
        f = acts[1, at].reshape(m, chans).astype(F32)
        inv_r, inv_f = inverse_norms(r, f, ones2, chans)
        nf = f * inv_f
        ld = lin * (r * inv_r - nf)
        q = dot((nf * ld).astype(BF16), ones1)
        if reps > 1:
            q = jnp.concatenate([q] * reps, axis=1)
        tap = (ld - nf * q) * (inv_f * scale)
        if up is not None:
            tap = tap + up(i0, chunk).reshape(m, chans)
        g = gelu_back(pres[at].reshape(m, chans)) * tap
        g = g.reshape((chunk,) + inner + (chans,))
        place = iota(g.shape, 0) + (start + i0)
        g = jnp.where((place >= 0) & (place < total_rows), g, 0.0)
        to = pl.ds(i0, chunk)
        if seg == 2:
            n = inner[1]
            for u in range(2):
                grads[to, u, 1 : n + 1] = g[:, u].astype(BF16)
            grads[to, 1, 0] = shifted(g[:, 1, n - 1], 1).astype(BF16)
            grads[to, 0, n + 1] = shifted(g[:, 0, 0], -1).astype(BF16)
        else:
            n = inner[0]
            grads[to, 1 : n + 1] = g.astype(BF16)
            grads[to, 0] = shifted(g[:, n - 1], 1).astype(BF16)
            grads[to, n + 1] = shifted(g[:, 0], -1).astype(BF16)

    count = own + 2 * halo
    if count == chunk:
        piece(0)
    else:
        pl.loop(0, count // chunk)(piece)


def back5_body(dims, a5, z5, w5, l5, i5, g5):
    H, L, HB, C1, C2, C3, C4, C5 = dims
    band = lax.axis_index("rows")
    own = HB // 16
    taps(5, a5, z5, g5, l5, band, HB, H, None, band * own, 2, own + 4)
    n = own + 2
    lhs = three(lambda dr, dc: g5[dr : dr + n, dc].reshape(n * L, C5))
    rhs = jnp.concatenate([w5[t * C4 : (t + 1) * C4, :] for t in range(8, -1, -1)], axis=1)
    i5[...] = (dot_t(lhs, rhs) * 0.25).reshape(n, 1, L, C4)


def spread_up(ref, axes):
    def load(i0, chunk):
        v = ref[pl.ds(i0 // 2, chunk // 2)]
        n, ph, length, chans = v.shape
        if axes:
            v = jnp.broadcast_to(v[:, None, None], (n, 2, 2, ph, length, chans))
            return v
        return jnp.broadcast_to(v[:, None, :, None], (n, 2, ph, 2, length, chans))

    return load


def back4_body(dims, a4, z4, w4, l4, i5, i4, g4):
    H, L, HB, C1, C2, C3, C4, C5 = dims
    band = lax.axis_index("rows")
    own, ph = (HB // 8, PH // 8)
    taps(4, a4, z4, g4, l4, band, HB, H, spread_up(i5, 0), band * own, 2, 2)
    n = own + 2
    lhs = three(lambda dr, dc: g4[dr : dr + n, dc : dc + ph].reshape(n * ph * L, C4))
    rhs = jnp.concatenate([w4[t * C3 : (t + 1) * C3, :] for t in range(8, -1, -1)], axis=1)
    i4[...] = (dot_t(lhs, rhs) * 0.25).reshape(n, ph, L, C3)


def back3_body(dims, a3, z3, w3, l3, i4, i3, g3):
    H, L, HB, C1, C2, C3, C4, C5 = dims
    band = lax.axis_index("rows")
    own, ph = (HB // 4, PH // 4)
    taps(3, a3, z3, g3, l3, band, HB, H, spread_up(i4, 0), ROWS3 - 2, 2, 4)
    n = own + 2
    lhs = three(lambda dr, dc: g3[dr : dr + n, dc : dc + ph].reshape(n * ph * L, C3))
    rhs = jnp.concatenate([w3[t * C2 : (t + 1) * C2, :] for t in range(8, -1, -1)], axis=1)
    i3[...] = (dot_t(lhs, rhs) * 0.25).reshape(n, ph, L, C2)


def back2_body(dims, a2, z2, w2t, l2, i3, i2, g2):
    H, L, HB, C1, C2, C3, C4, C5 = dims
    band = lax.axis_index("rows")
    own, ph = (HB // 2, PH // 4)
    taps(2, a2, z2, g2, l2, band, HB, H, spread_up(i3, 1), ROWS2 - 2, 2, 4)
    step = (own + 2) // 2
    for r0 in (0, step):
        lhs = jnp.concatenate(
            [
                g2[r0 + dr : r0 + dr + step, 1 - j % 2, (j + 1) // 2 : (j + 1) // 2 + ph].reshape(
                    step * ph * L, C2
                )
                for dr in range(3)
                for j in range(4)
            ],
            axis=1,
        )
        out = (dot_t(lhs, w2t[...]) * 0.25).reshape(step, ph, L, 2 * LANES)
        for u in range(2):
            i2[r0 : r0 + step, u] = out[..., u * LANES : (u + 1) * LANES]


def back1_body(dims, a1, z1, r1, l1, i2, grad_ref, g1):
    H, L, HB, C1, C2, C3, C4, C5 = dims
    band = lax.axis_index("rows")
    ph = PH // 4

    def up(i0, chunk):
        v = i2[pl.ds(i0 // 2, chunk // 2 + 1)]
        v = jnp.stack([v[:, q % 2, q // 2] for q in range(2 * ph)], axis=1)
        return jnp.stack([v[(j + 1) // 2] for j in range(chunk)])

    taps(1, a1, z1, g1, l1, band, HB, H, up, ROWS1 - 1, 1, 6)
    lhs = jnp.concatenate(
        [g1[dr : dr + HB, j].reshape(HB * L, LANES) for dr in range(3) for j in range(PH // 2 + 2)],
        axis=1,
    )
    gin = dot_t(lhs, r1[...])
    high = gin.astype(BF16)
    split = jnp.concatenate([high.astype(F32), gin - high.astype(F32)], axis=1).astype(BF16)
    width = PH * L
    sel_row = iota((LANES, width), 0) % HALF
    sel_col = iota((LANES, width), 1) % PH
    shape = (HB * L, width)
    inside = iota(shape, 1) // PH == iota(shape, 0) % L
    for ch in range(3):
        pick = jnp.where(sel_row == sel_col * 3 + ch, 1.0, 0.0).astype(BF16)
        wide = jnp.where(inside, dot(split, pick), 0.0)
        grad_ref[ch] = jnp.sum(wide.reshape(HB, L, width), axis=1)


ROWS1, ROWS2, ROWS3, ROWS4 = (8, 4, 4, 4)


def frame_work(x, c1, c2, b1, convs, biases, linears, HB):
    H, L, _ = x.shape
    C1, C2, C3, C4, C5 = [c.shape[-1] for c in convs]
    dims = (H, L, HB, C1, C2, C3, C4, C5)
    ph2, ph3, ph4 = (PH // 2, PH // 4, PH // 8)
    V = pltpu.VMEM
    far = [c.reshape(-1, c.shape[-1]) for c in convs[2:]]
    far += [v.reshape(1, -1) for v in (*biases[1:], *linears)]
    w1, r1, w2, w2t = call(
        weights_body,
        (
            V((4 * HALF, PH * HALF), BF16),
            V((HALF, 3 * (ph2 + 2) * LANES), BF16),
            V((12 * C1, 2 * C2), BF16),
            V((4 * C1, 12 * C2), BF16),
        ),
        (c1, c2, b1),
        "weights",
        (V((3, HALF, LANES), F32), V((8, LANES), F32)),
        limit=8,
    )
    acts = (
        (HB + 3 * ROWS1, ph2, L, LANES),
        (HB // 2 + 3 * ROWS2, 2, ph3, L, C2),
        (HB // 4 + 3 * ROWS3, ph3, L, C3),
        (H // 8 + 4, ph4, L, C4),
        (H // 16 + 4, 1, L, C5),
    )
    outs = (V((8, LANES), F32),)
    outs += tuple(V((2,) + s, BF16) for s in acts) + tuple(V(s, F32) for s in acts)
    outs += tuple(V(v.shape, v.dtype) for v in far)
    loss, a1, a2, a3, a4, a5, z1, z2, z3, z4, z5, w3, w4, w5, *vecs = call(
        functools.partial(forward_body, dims),
        outs,
        (x, w1, w2),
        "forward",
        (
            V((2, H, L, 2 * LANES), BF16),
            V((2, H // 2 + 2, ph2, L, LANES), BF16),
            V((2, H // 4 + 2, ph3 + 2, L, C2), BF16),
            V((2, H // 8 + 2, ph4 + 2, L, C3), BF16),
            V((2, H // 16 + 2, 3, L, C4), BF16),
            pltpu.SemaphoreType.DMA((12,)),
        ),
        limit=24,
        far=far,
    )
    l = vecs[4:]
    n1, n2, n3, n4, n5 = (HB + 2, HB // 2 + 4, HB // 4 + 4, HB // 8 + 4, HB // 16 + 4)

    def step(body, name, ins, out, scratch, flops):
        return call(functools.partial(body, dims), out, ins, name, (V(scratch, BF16),), 12, flops)

    def back5(_):
        return step(
            back5_body, "back5", (a5, z5, w5, l[4]), V((n5 - 2, 1, L, C4), F32), (n5, 3, L, C5), FL
        )

    def back4(i5):
        return step(
            back4_body, "back4", (a4, z4, w4, l[3], i5), V((n4 - 2, ph4, L, C3), F32),
            (n4, ph4 + 2, L, C4), FL,
        )

    def back3(i4):
        return step(
            back3_body, "back3", (a3, z3, w3, l[2], i4), V((n3 - 2, ph3, L, C2), F32),
            (n3, ph3 + 2, L, C3), FL,
        )

    def back2(i3):
        return step(
            back2_body, "back2", (a2, z2, w2t, l[1], i3), V((n2 - 2, 2, ph3, L, LANES), F32),
            (n2, 2, ph3 + 2, L, C2), FL,
        )

    def back1(i2):
        return step(
            back1_body, "back1", (a1, z1, r1, l[0], i2),
            jax.ShapeDtypeStruct((3, HB, L * PH), F32), (n1, ph2 + 2, L, LANES), FL,
        )

    return loss, (back5, back4, back3, back2, back1)


FL = 10**9


def on_device(real_frames, fake_frames, *params):
    convs, biases, linears = (params[0:5], params[5:10], params[10:15])
    frames, _, band_rows, width = real_frames.shape
    bands = lax.axis_size("rows")
    frame_total = frames * lax.axis_size("dp")
    work = []
    for n in range(frames):
        c1, c2, b1 = (convs[0], convs[1], biases[0].reshape(1, -1))
        c2 = c2.reshape(9, *c2.shape[2:])
        x, c1, c2, b1 = prep(real_frames[n], fake_frames[n], c1, c2, b1)
        x = lax.all_gather(x, "rows", axis=0, tiled=True)
        work.append(frame_work(x, c1, c2, b1, convs, biases, linears, band_rows))
    total = functools.reduce(jnp.add, [loss for loss, _ in work])
    hops = []
    for axis in ("rows", "dp"):
        hop = 1
        while hop < lax.axis_size(axis):
            hops.append((axis, hop))
            hop *= 2
    states = [None] * frames
    for stage in range(max(5, len(hops))):
        if stage < len(hops):
            axis, hop = hops[stage]
            pairs = [(i, i ^ hop) for i in range(lax.axis_size(axis))]
            other = lax.ppermute(total, axis, pairs)
        if stage < 5:
            states = [steps[stage](s) for s, (_, steps) in zip(states, work)]
        if stage < len(hops):
            total, other, states = lax.optimization_barrier((total, other, states))
            total = total + other
    counts = [frame_total * (band_rows * bands >> s) * (width >> s) for s in range(5)]
    losses = jnp.sum(total, axis=1)[0:5] * jnp.array([1.0 / c for c in counts], F32)
    return (losses, jnp.stack(states))


def solution(mesh):
    frame = P("dp", None, "rows", None)
    return jax.shard_map(
        on_device,
        mesh=mesh,
        in_specs=(frame, frame) + (P(),) * 15,
        out_specs=(P(), frame),
        check_vma=False,
    )
```

profile of v0, /device:TPU:0, one launch (start us, length us, event | category | flops | bytes accessed | tf_op | source)
XLA Modules:
  0.0 46.3 jit_solution(9371479410197968211)
XLA Ops:
  0.6 1.6 %prep.1 = (bf16[16,16,128]{2,1,0:T(8,128)(2,1)S(1)}, bf16[3,3,3,64]{3,2,1,0:T(4,128)(2,1)S(1)}, bf16[9,64,128]{2,1,0:T(8,128)(2,1)S(1)}, f32[1,64]{1,0:T(1,128)S(1)}) custom-call(bf16[3,16,256]{2,1,0:T(8,128)(2,1)} %bitcast.22, bf16[3,16,256]{2,1,0:T(8,128)(2,1)} %bitcast.23, bf16[3,3,3,64]{3,2,1,0:T(4,128)(2,1)} %c1_hbm.1, bf16[9,64,128]{2,1,0:T(8,128)(2,1)} %bitcast.20, ...), custom_call_target="tpu_custom_call" | custom-call | tf_op jit(solution)/shard_map/prep/pallas_call | solution.py:65
  2.2 7.2 %all_gather.3.refs_12_ = bf16[64,16,128]{2,1,0:T(8,128)(2,1)S(1)} all-gather(bf16[16,16,128]{2,1,0:T(8,128)(2,1)S(1)} %get-tuple-element.44), channel_id=1, replica_groups=mesh['dp'=8,'rows'=4] {'rows'}, dimensions={0}, use_global_device_ids=true | all-gather | bytes 327680 | tf_op jit(solution)/shard_map/all_gather | solution.py:664
  9.5 0.3 weights.1
  9.8 16.1 %forward.1 = (f32[8,128]{1,0:T(8,128)S(1)}, bf16[2,40,8,16,128]{4,3,2,1,0:T(8,128)(2,1)S(1)}, bf16[2,20,2,4,16,128]{5,4,3,2,1,0:T(8,128)(2,1)S(1)}, bf16[2,16,4,...) custom-call(bf16[1152,256]{1,0:T(8,128)(2,1)} %bitcast.19, ...), custom_call_target="tpu_custom_call" | custom-call | tf_op jit(solution)/shard_map/forward/pallas_call | solution.py:65
  25.9 0.4 collective-permute-start
  26.4 1.8 %back5.1.i5 = f32[3,1,16,512]{3,2,1,0:T(8,128)S(1)} custom-call(bf16[2,8,1,16,512]{4,3,2,1,0:T(8,128)(2,1)S(1)} %get-tuple-element.51.a5, f32[8,1,16,512]{3,2,1,0:T(8,128)S(1)} %get-tuple-element.52.z5, bf16[4608,512]{1,0:T(8,128)(2,1)S(1)} %get-tuple-element.53.w5, f32[1,512]{1,0:T(1,128)S(1)} %get-tuple-element.54.l5), custom_call_target="tpu_custom_call" | custom-call | flops 1000000000 | tf_op jit(solution)/shard_map/back5/pallas_call | solution.py:65
  28.2 0.0 collective-permute-done
  28.2 1.6 %collective-permute-start.1 = (f32[8,128]{1,0:T(8,128)S(1)}, f32[8,128]{1,0:T(8,128)S(1)}, u32[]{:S(2)}, u32[]{:S(2)}) collective-permute-start(f32[8,128]{1,0:T(8,128)S(1)} %add.15), channel_id=1, source_target_pairs={{0,2},{1,3},{2,0},{3,1},{4,6},{5,7},{6,4},{7,5},{8,10},{9,11},{10,... | collective-permute-start | bytes 12296 | tf_op jit(solution)/shard_map/ppermute | solution.py:678
  29.8 2.1 %back4.1.i4 = f32[4,2,16,256]{3,2,1,0:T(8,128)S(1)} custom-call(bf16[2,12,2,16,512]{4,3,2,1,0:T(8,128)(2,1)S(1)} %get-tuple-element.57.a4, f32[12,2,16,512]{3,2,1,0:T(8,128)S(1)} %get-tuple-element.58.z4, bf16[2304,512]{1,0:T(8,128)(2,1)S(1)} %get-tuple-element.59.w4, f32[1,512]{1,0:T(1,128)S(1)} %get-tuple-element.60.l4, f32[3,1,16,512]{3,2,1,0:T(8,128)S(1)} %back5.1.i5), custom_call_target="tpu_custom_call" | custom-call | flops 1000000000 | tf_op jit(solution)/shard_map/back4/pallas_call | solution.py:65
  31.9 0.0 collective-permute-done.1
  32.0 1.6 %collective-permute-start.2 = (f32[8,128]{1,0:T(8,128)S(1)}, f32[8,128]{1,0:T(8,128)S(1)}, u32[]{:S(2)}, u32[]{:S(2)}) collective-permute-start(f32[8,128]{1,0:T(8,128)S(1)} %add.16), channel_id=1, source_target_pairs={{0,4},{4,0},{8,12},{12,8},{16,20},{20,16},{24,28},{28,24},{1,5},{5... | collective-permute-start | bytes 12296 | tf_op jit(solution)/shard_map/ppermute | solution.py:678
  33.5 1.6 %back3.1.i3 = f32[6,4,16,128]{3,2,1,0:T(8,128)S(1)} custom-call(bf16[2,16,4,16,256]{4,3,2,1,0:T(8,128)(2,1)S(1)} %get-tuple-element.64.a3, f32[16,4,16,256]{3,2,1,0:T(8,128)S(1)} %get-tuple-element.65.z3, bf16[1152,256]{1,0:T(8,128)(2,1)S(1)} %get-tuple-element.66.w3, f32[1,256]{1,0:T(1,128)S(1)} %get-tuple-element.67.l3, f32[4,2,16,256]{3,2,1,0:T(8,128)S(1)} %back4.1.i4), custom_call_target="tpu_custom_call" | custom-call | flops 1000000000 | tf_op jit(solution)/shard_map/back3/pallas_call | solution.py:65
  35.2 0.5 collective-permute-done.2
  35.6 1.6 %collective-permute-start.3 = (f32[8,128]{1,0:T(8,128)S(1)}, f32[8,128]{1,0:T(8,128)S(1)}, u32[]{:S(2)}, u32[]{:S(2)}) collective-permute-start(f32[8,128]{1,0:T(8,128)S(1)} %add.17), channel_id=1, source_target_pairs={{0,8},{4,12},{8,0},{12,4},{16,24},{20,28},{24,16},{28,20},{1,9},{5... | collective-permute-start | bytes 12296 | tf_op jit(solution)/shard_map/ppermute | solution.py:678
  37.2 2.1 %back2.1.i2 = f32[10,2,4,16,128]{4,3,2,1,0:T(8,128)S(1)} custom-call(bf16[2,20,2,4,16,128]{5,4,3,2,1,0:T(8,128)(2,1)S(1)} %get-tuple-element.71.a2, f32[20,2,4,16,128]{4,3,2,1,0:T(8,128)S(1)} %get-tuple-element.72.z2, bf16[256,1536]{1,0:T(8,128)(2,1)S(1)} %get-tuple-element.73.w2t, f32[1,128]{1,0:T(1,128)S(1)} %get-tuple-element.74.l2, ...), custom_call_target="tpu_custom_call" | custom-call | flops 1000000000 | tf_op jit(solution)/shard_map/back2/pallas_call | solution.py:65
  39.3 0.0 collective-permute-done.3
  39.4 2.6 %collective-permute-start.4 = (f32[8,128]{1,0:T(8,128)S(1)}, f32[8,128]{1,0:T(8,128)S(1)}, u32[]{:S(2)}, u32[]{:S(2)}) collective-permute-start(f32[8,128]{1,0:T(8,128)S(1)} %add.18), channel_id=1, source_target_pairs={{0,16},{4,20},{8,24},{12,28},{16,0},{20,4},{24,8},{28,12},{1,17},{... | collective-permute-start | bytes 12296 | tf_op jit(solution)/shard_map/ppermute | solution.py:678
  42.0 0.0 copy-start
  42.0 3.7 %back1.1 = f32[3,16,256]{2,1,0:T(8,128)} custom-call(bf16[2,40,8,16,128]{4,3,2,1,0:T(8,128)(2,1)S(1)} %get-tuple-element.78.a1, f32[40,8,16,128]{3,2,1,0:T(8,128)S(1)} %get-tuple-element.79.z1, bf16[64,3840]{1,0:T(8,128)(2,1)S(1)} %get-tuple-element.80.r1, f32[1,64]{1,0:T(1,128)S(1)} %get-tuple-element.81.l1, f32[10,2,4,16,128]{4,3,2,1,0:T(8,128)S(1)} %back2.1.i2), custom_call_target="tpu_custom_call" | custom-call | flops 1000000000 | tf_op jit(solution)/shard_map/back1/pallas_call | solution.py:65
  45.7 0.0 collective-permute-done.4
  45.7 0.1 add_reduce_fusion
  45.8 0.0 copy-done
  45.8 0.5 %slice_multiply_fusion = f32[5]{0:T(128)} fusion(f32[5]{0:T(128)S(1)} %copy-done, f32[8]{0:T(128)S(1)} %add_reduce_fusion), kind=kLoop, calls=%fused_computation.1 | loop fusion | flops 5 | bytes 60 | tf_op jit(solution)/shard_map/mul | solution.py:685
  (4 shorter events, 0.0 us)
Async XLA Ops:
  25.9 2.3 %collective-permute-start = (f32[8,128]{1,0:T(8,128)S(1)}, f32[8,128]{1,0:T(8,128)S(1)}, u32[]{:S(2)}, u32[]{:S(2)}) collective-permute-start(f32[8,128]{1,0:T(8,128)S(1)} %get-tuple-element.55), channel_id=1, source_target_pairs={{0,1},{1,0},{2,3},{3,2},{4,5},{5,4},{6,7},{7,6},{8,9},{9,8},{10,11... | collective-permute-start | bytes 12296 | tf_op jit(solution)/shard_map/ppermute | solution.py:678
  28.2 3.7 %collective-permute-start.1 = (f32[8,128]{1,0:T(8,128)S(1)}, f32[8,128]{1,0:T(8,128)S(1)}, u32[]{:S(2)}, u32[]{:S(2)}) collective-permute-start(f32[8,128]{1,0:T(8,128)S(1)} %add.15), channel_id=1, source_target_pairs={{0,2},{1,3},{2,0},{3,1},{4,6},{5,7},{6,4},{7,5},{8,10},{9,11},{10,... | collective-permute-start | bytes 12296 | tf_op jit(solution)/shard_map/ppermute | solution.py:678
  32.0 3.7 %collective-permute-start.2 = (f32[8,128]{1,0:T(8,128)S(1)}, f32[8,128]{1,0:T(8,128)S(1)}, u32[]{:S(2)}, u32[]{:S(2)}) collective-permute-start(f32[8,128]{1,0:T(8,128)S(1)} %add.16), channel_id=1, source_target_pairs={{0,4},{4,0},{8,12},{12,8},{16,20},{20,16},{24,28},{28,24},{1,5},{5... | collective-permute-start | bytes 12296 | tf_op jit(solution)/shard_map/ppermute | solution.py:678
  35.6 3.7 %collective-permute-start.3 = (f32[8,128]{1,0:T(8,128)S(1)}, f32[8,128]{1,0:T(8,128)S(1)}, u32[]{:S(2)}, u32[]{:S(2)}) collective-permute-start(f32[8,128]{1,0:T(8,128)S(1)} %add.17), channel_id=1, source_target_pairs={{0,8},{4,12},{8,0},{12,4},{16,24},{20,28},{24,16},{28,20},{1,9},{5... | collective-permute-start | bytes 12296 | tf_op jit(solution)/shard_map/ppermute | solution.py:678
  39.4 6.3 %collective-permute-start.4 = (f32[8,128]{1,0:T(8,128)S(1)}, f32[8,128]{1,0:T(8,128)S(1)}, u32[]{:S(2)}, u32[]{:S(2)}) collective-permute-start(f32[8,128]{1,0:T(8,128)S(1)} %add.18), channel_id=1, source_target_pairs={{0,16},{4,20},{8,24},{12,28},{16,0},{20,4},{24,8},{28,12},{1,17},{... | collective-permute-start | bytes 12296 | tf_op jit(solution)/shard_map/ppermute | solution.py:678
  42.0 3.8 %copy-start = (f32[5]{0:T(128)S(1)}, f32[5]{0:T(128)}, u32[]{:S(2)}) copy-start(f32[5]{0:T(128)} %constant.4.clone) | copy-start | bytes 64
where the time goes:
time: 46.5 us; the launch traced here: 46.3 us
  Pallas kernels  29.4 us (63%)
  starting transfers between devices  7.81 us (17%)
  blocking collectives  7.22 us (16%)
  between operations  0.74 us (2%)
  other arithmetic  0.65 us (1%)
    pallas_call x8, Pallas kernels, call(): pl.pallas_call(body, out_shape=outs, in_specs=[HBM] * len(far) + [VM] * l...  29.4 us
    ppermute x5, starting transfers between devices, on_device(): other = lax.ppermute(total, axis, pairs)  7.81 us
    all_gather x1, blocking collectives, on_device(): x = lax.all_gather(x, 'rows', axis=0, tiled=True)  7.22 us
  transfers between devices with their start and end apart: 5, of which 1 were waited for; matrix products, arithmetic and copies ran while one was open for 0% of the time, Pallas kernels for 25%

commit v1 on v0

--- a/solution.py
+++ b/solution.py
@@ -163,9 +163,9 @@
             blk = jnp.where(
                 lo, pltpu.roll(b, s0, 0) if s0 else b, pltpu.roll(b, s1, 0) if s1 else b
             )
-            k = (dr * (PH // 2 + 2) + j) * LANES
-            r1[:, k : k + LANES] = blk.astype(BF16)
+            r1[dr * HALF : (dr + 1) * HALF, j * LANES : (j + 1) * LANES] = blk.astype(BF16)
     w1[3 * HALF : 4 * HALF, :] = jnp.zeros((HALF, w1.shape[1]), BF16)
+    r1[3 * HALF : 4 * HALF, :] = jnp.zeros((HALF, r1.shape[1]), BF16)
     w2[...] = jnp.zeros(w2.shape, BF16)
     w2t[...] = jnp.zeros(w2t.shape, BF16)
     slot = (2, 0, 1, 3)
@@ -175,7 +175,7 @@
             back = c2_ref[(2 - dr) * 3 + 2 - dc]
             for u in range(2):
                 k = (dr * 4 + slot[dc + u]) * C1
-                w2[k : k + C1, u * C2 : (u + 1) * C2] = blk
+                w2[k : k + C1, u * C2 : (u + 1) * C2] = (blk.astype(F32) * 0.125).astype(BF16)
                 k = (dr * 4 + dc + u) * C2
                 for d in range(2):
                     n = (u * 2 + d) * C1
@@ -217,15 +217,16 @@
     dims,
     *refs,
 ):
+    H, L, HB, C1, C2, C3, C4, C5 = dims
     far, refs = (refs[0:12], refs[12:])
-    x_ref, w1, w2, loss_ref, a1, a2, a3, a4, a5, z1, z2, z3, z4, z5 = refs[0:14]
-    near, refs = (refs[14:26], refs[26:])
-    w3, w4, w5, b2_ref, b3_ref, b4_ref, b5_ref, l1_ref, l2_ref, l3_ref, l4_ref, l5_ref = near
-    xk, p1, p2, p3, p4, sems = refs
+    blocks, refs = (refs[0 : H // HB], refs[H // HB :])
+    w1, w2, loss_ref, t1, t2, t3, t4, t5, z1, z2, z3, z4, z5 = refs[0:13]
+    near, refs = (refs[13:25], refs[25:])
+    w3, w4, w5, b2_ref, b3_ref, b4_ref, b5_ref, *l_refs = near
+    xs, xk, p1, p2, p3, p4, a1, a2, a3, a4, a5, sems = refs
     copies = [pltpu.make_async_copy(a, b, sems.at[i]) for i, (a, b) in enumerate(zip(far, near))]
     for copy in copies[3:] + copies[:3]:
         copy.start()
-    H, L, HB, C1, C2, C3, C4, C5 = dims
     ph2, ph3, ph4 = (PH // 2, PH // 4, PH // 8)
     band = lax.axis_index("rows")
     for p in (p1, p2, p3, p4):
@@ -234,21 +235,17 @@
             p[img, 0] = jnp.zeros(p.shape[2:], BF16)
             p[img, n - 1] = jnp.zeros(p.shape[2:], BF16)
 
-    x = x_ref[...].astype(F32)
-    xr = pltpu.roll(x.reshape(H * L, LANES), HALF, 1).reshape(H, L, LANES)
-    zero = jnp.zeros((1, L, LANES), F32)
+    xs[0] = jnp.zeros((L, LANES), BF16)
+    xs[H + 1] = jnp.zeros((L, LANES), BF16)
+    for m, block in enumerate(blocks):
+        xs[pl.ds((band ^ m) * HB + 1, HB)] = block[...]
+    x = xs[...].astype(F32)
+    xr = pltpu.roll(x.reshape((H + 2) * L, LANES), HALF, 1).reshape(H + 2, L, LANES)
     lo3 = low_half((H, L, LANES))
-
-    def above(v):
-        return jnp.concatenate([zero, v[: H - 1]], axis=0)
-
-    def below(v):
-        return jnp.concatenate([v[1:], zero], axis=0)
-
-    xk[0, :, :, 0:LANES] = jnp.where(lo3, above(x), xr).astype(BF16)
-    xk[0, :, :, LANES : 2 * LANES] = below(x).astype(BF16)
-    xk[1, :, :, 0:LANES] = jnp.where(lo3, above(xr), x).astype(BF16)
-    xk[1, :, :, LANES : 2 * LANES] = below(xr).astype(BF16)
+    xk[0, :, :, 0:LANES] = jnp.where(lo3, x[0:H], xr[1 : H + 1]).astype(BF16)
+    xk[0, :, :, LANES : 2 * LANES] = x[2 : H + 2].astype(BF16)
+    xk[1, :, :, 0:LANES] = jnp.where(lo3, xr[0:H], x[1 : H + 1]).astype(BF16)
+    xk[1, :, :, LANES : 2 * LANES] = xr[2 : H + 2].astype(BF16)
 
     def keep(r0, rows, size, first):
         place = r0 - first
@@ -256,7 +253,7 @@
 
     rows = ROWS1
 
-    @pl.loop(0, H // rows)
+    @pl.loop(0, H // rows, unroll=2)
     def _(step):
         r0 = step * rows
         kept = keep(r0, rows, HB + 2 * rows, band * HB - rows)
@@ -274,7 +271,7 @@
                         z1[kept, n * 2 + i] = h[:, lanes].reshape(rows, L, LANES)
                     pair = part.reshape(rows // 2, 2, L, LANES)
                     s = (pair[:, 0] + pair[:, 1]).reshape(rows // 2 * L, LANES)
-                    s = ((s + pltpu.roll(s, HALF, 1)) * 0.125).reshape(rows // 2, L, LANES)
+                    s = (s + pltpu.roll(s, HALF, 1)).reshape(rows // 2, L, LANES)
                     half = slice(i * HALF, (i + 1) * HALF)
                     p1[img, at, n, :, half] = s.astype(BF16)[..., half]
                     q = n * 2 + i
@@ -289,11 +286,21 @@
     for copy in copies[3:]:
         copy.wait()
 
-    rows2 = ROWS2
+    rows2, rows3, rows4 = (ROWS2, ROWS3, ROWS4)
+    loss_ref[...] = jnp.zeros(loss_ref.shape, F32)
+    places = (rows - 1, rows2 - 2, rows3 - 2, band * (HB // 8), band * (HB // 16))
+
+    def tap(seg):
+        s = seg - 1
+        acts = (a1, a2, a3, a4, a5)[s]
+        taps(seg, acts, (t1, t2, t3, t4, t5)[s], l_refs[s], loss_ref, HB >> s, places[s])
+
+    for copy in copies[:3]:
+        copy.wait()
+    tap(1)
     bias = jnp.concatenate([b2_ref[...]] * 2, axis=1) * 0.5
 
-    @pl.loop(0, H // 2 // rows2)
-    def _(step):
+    for step in range(H // 2 // rows2):
         r0 = step * rows2
         kept = keep(r0, rows2, HB // 2 + 2 * rows2, band * (HB // 2) - rows2)
         for img in range(2):
@@ -317,12 +324,10 @@
             s = (act[:, 0:C2] + act[:, C2 : 2 * C2]).reshape(rows2 // 2, 2, ph3, L, C2)
             pooled_into(p2, img, r0 // 2, (s[:, 0] + s[:, 1]) * 0.125)
 
-    copies[0].wait()
-    rows3 = ROWS3
+    tap(2)
     bias3 = b3_ref[...] * 0.5
 
-    @pl.loop(0, H // 4 // rows3)
-    def _(step):
+    for step in range(H // 4 // rows3):
         r0 = step * rows3
         kept = keep(r0, rows3, HB // 4 + 2 * rows3, band * (HB // 4) - rows3)
         for img in range(2):
@@ -340,30 +345,42 @@
             pooled = (pair[:, 0, :, 0] + pair[:, 0, :, 1]) + (pair[:, 1, :, 0] + pair[:, 1, :, 1])
             pooled_into(p3, img, r0 // 2, pooled * 0.125)
 
-    copies[1].wait()
-    rows4 = ROWS4
+    tap(3)
     bias4 = b4_ref[...] * 0.5
 
-    @pl.loop(0, H // 8 // rows4)
-    def _(step):
+    for step in range(H // 8 // rows4):
         r0 = step * rows4
-        for img in range(2):
-            lhs = three(
-                lambda dr, dc: p3[img, pl.ds(r0 + dr, rows4), dc : dc + ph4].reshape(
-                    rows4 * ph4 * L, C3
+        lhs = jnp.concatenate(
+            [
+                three(
+                    lambda dr, dc, img=img: p3[
+                        img, pl.ds(r0 + dr, rows4), dc : dc + ph4
+                    ].reshape(rows4 * ph4 * L, C3)
                 )
-            )
-            h = dot(lhs, w4[...]) + bias4
-            act = gelu(h)
-            at = pl.ds(r0 + 2, rows4)
-            a4[img, at] = act.astype(BF16).reshape(rows4, ph4, L, C4)
-            if img:
-                z4[at] = h.reshape(rows4, ph4, L, C4)
-            pair = act.reshape(rows4 // 2, 2, ph4, L, C4)
-            pooled = (pair[:, 0, 0] + pair[:, 0, 1]) + (pair[:, 1, 0] + pair[:, 1, 1])
-            pooled_into(p4, img, r0 // 2, (pooled * 0.125)[:, None])
-
-    copies[2].wait()
+                for img in range(2)
+            ],
+            axis=0,
+        )
+        m = rows4 * ph4 * L
+        at = pl.ds(r0 + 2, rows4)
+        to = pl.ds(r0 // 2 + 1, rows4 // 2)
+        for n in range(0, C4, 256):
+            lanes = slice(n, n + 256)
+            both = dot(lhs, w4[:, lanes]) + bias4[:, lanes]
+            for img in range(2):
+                h = both[img * m : (img + 1) * m]
+                act = gelu(h)
+                a4[img, at, :, :, lanes] = act.astype(BF16).reshape(rows4, ph4, L, 256)
+                if img:
+                    z4[at, :, :, lanes] = h.reshape(rows4, ph4, L, 256)
+                pair = act.reshape(rows4 // 2, 2, ph4, L, 256)
+                pooled = (pair[:, 0, 0] + pair[:, 0, 1]) + (pair[:, 1, 0] + pair[:, 1, 1])
+                pooled = pooled * 0.125
+                p4[img, to, 1, :, lanes] = pooled.astype(BF16)
+                p4[img, to, 0, :, lanes] = shifted(pooled, 1).astype(BF16)
+                p4[img, to, 2, :, lanes] = shifted(pooled, -1).astype(BF16)
+
+    tap(4)
     h5 = H // 16
     lhs = jnp.concatenate(
         [
@@ -377,47 +394,16 @@
     for img in range(2):
         a5[img, 2 : 2 + h5, 0] = act[img * h5 * L : (img + 1) * h5 * L].reshape(h5, L, C5)
     z5[2 : 2 + h5, 0] = h[h5 * L :].reshape(h5, L, C5)
-
-    loss_ref[...] = jnp.zeros(loss_ref.shape, F32)
-    places = (rows, rows2, rows3, 2 + band * (HB // 8), 2 + band * (HB // 16))
-    chunks = (4, 4, 4, 2, 1)
-    for s, (acts, l_ref) in enumerate(
-        ((a1, l1_ref), (a2, l2_ref), (a3, l3_ref), (a4, l4_ref), (a5, l5_ref))
-    ):
-        chans = acts.shape[-1]
-        ones2 = ones_for(s + 1, chans)
-        own, chunk = (HB >> s, chunks[s])
-        m = chunk * math.prod(acts.shape[2:-1])
-        lin = l_ref[...]
-        if s == 0:
-            lin = jnp.concatenate([lin, lin], axis=1)
-
-        def piece(k, s=s, acts=acts, ones2=ones2, chunk=chunk, m=m, chans=chans, lin=lin):
-            at = pl.ds(places[s] + k * chunk, chunk)
-            r = acts[0, at].reshape(m, chans).astype(F32)
-            f = acts[1, at].reshape(m, chans).astype(F32)
-            inv_r, inv_f = inverse_norms(r, f, ones2, chans)
-            d = r * inv_r - f * inv_f
-            part = jnp.sum(d * d, axis=0, keepdims=True) * lin
-            acc = part[:, 0:LANES]
-            for j in range(1, chans // LANES):
-                acc = acc + part[:, j * LANES : (j + 1) * LANES]
-            loss_ref[s : s + 1, :] += acc
-
-        if own == chunk:
-            piece(0)
-        else:
-            pl.loop(0, own // chunk)(piece)
-
-
-def taps(seg, acts, pres, grads, l_ref, band, HB, H, up, local, halo, chunk):
+    tap(5)
+
+
+def taps(seg, acts, grads, l_ref, loss_ref, own, local):
     chans = acts.shape[-1]
     inner = acts.shape[2:-1]
+    halo = 1 if seg == 1 else 2
+    count = own + 2 * halo
+    chunk = TAP_ROWS[seg - 1] or count
     m = chunk * math.prod(inner)
-    L = inner[-1]
-    own = HB >> (seg - 1)
-    total_rows = H >> (seg - 1)
-    start = band * own - halo
     scale = -2.0 * 4.0 ** (seg - 1)
     ones2 = ones_for(seg, chans)
     ones1 = ones2[0:LANES, 0:LANES] if seg == 1 else jnp.ones((chans, LANES), BF16)
@@ -433,16 +419,41 @@
         f = acts[1, at].reshape(m, chans).astype(F32)
         inv_r, inv_f = inverse_norms(r, f, ones2, chans)
         nf = f * inv_f
-        ld = lin * (r * inv_r - nf)
+        d = r * inv_r - nf
+        ld = lin * d
         q = dot((nf * ld).astype(BF16), ones1)
         if reps > 1:
             q = jnp.concatenate([q] * reps, axis=1)
         tap = (ld - nf * q) * (inv_f * scale)
+        grads[pl.ds(i0, chunk)] = tap.reshape((chunk,) + inner + (chans,))
+        mapped = (ld * d).reshape((chunk,) + inner + (chans,))
+        place = iota(mapped.shape, 0) + i0
+        mapped = jnp.where((place >= halo) & (place < halo + own), mapped, 0.0)
+        part = jnp.sum(mapped.reshape(m, chans), axis=0, keepdims=True)
+        acc = part[:, 0:LANES]
+        for j in range(1, reps):
+            acc = acc + part[:, j * LANES : (j + 1) * LANES]
+        loss_ref[seg - 1 : seg, :] += acc
+
+    for k in range(count // chunk):
+        piece(k)
+
+
+def pre_grads(seg, tap_ref, pres, grads, band, HB, H, up, local, halo, chunk):
+    chans = pres.shape[-1]
+    inner = pres.shape[1:-1]
+    own = HB >> (seg - 1)
+    total_rows = H >> (seg - 1)
+    start = band * own - halo
+    shape = (chunk,) + inner + (chans,)
+
+    def piece(k):
+        i0 = k * chunk
+        g = tap_ref[pl.ds(i0, chunk)]
         if up is not None:
-            tap = tap + up(i0, chunk).reshape(m, chans)
-        g = gelu_back(pres[at].reshape(m, chans)) * tap
-        g = g.reshape((chunk,) + inner + (chans,))
-        place = iota(g.shape, 0) + (start + i0)
+            g = g + up(i0, chunk).reshape(shape)
+        g = gelu_back(pres[pl.ds(local + i0, chunk)]) * g
+        place = iota(shape, 0) + (start + i0)
         g = jnp.where((place >= 0) & (place < total_rows), g, 0.0)
         to = pl.ds(i0, chunk)
         if seg == 2:
@@ -464,11 +475,11 @@
         pl.loop(0, count // chunk)(piece)
 
 
-def back5_body(dims, a5, z5, w5, l5, i5, g5):
+def back5_body(dims, t5, z5, w5, i5, g5):
     H, L, HB, C1, C2, C3, C4, C5 = dims
     band = lax.axis_index("rows")
     own = HB // 16
-    taps(5, a5, z5, g5, l5, band, HB, H, None, band * own, 2, own + 4)
+    pre_grads(5, t5, z5, g5, band, HB, H, None, band * own, 2, own + 4)
     n = own + 2
     lhs = three(lambda dr, dc: g5[dr : dr + n, dc].reshape(n * L, C5))
     rhs = jnp.concatenate([w5[t * C4 : (t + 1) * C4, :] for t in range(8, -1, -1)], axis=1)
@@ -487,33 +498,33 @@
     return load
 
 
-def back4_body(dims, a4, z4, w4, l4, i5, i4, g4):
+def back4_body(dims, t4, z4, w4, i5, i4, g4):
     H, L, HB, C1, C2, C3, C4, C5 = dims
     band = lax.axis_index("rows")
     own, ph = (HB // 8, PH // 8)
-    taps(4, a4, z4, g4, l4, band, HB, H, spread_up(i5, 0), band * own, 2, 2)
+    pre_grads(4, t4, z4, g4, band, HB, H, spread_up(i5, 0), band * own, 2, own + 4)
     n = own + 2
     lhs = three(lambda dr, dc: g4[dr : dr + n, dc : dc + ph].reshape(n * ph * L, C4))
     rhs = jnp.concatenate([w4[t * C3 : (t + 1) * C3, :] for t in range(8, -1, -1)], axis=1)
     i4[...] = (dot_t(lhs, rhs) * 0.25).reshape(n, ph, L, C3)
 
 
-def back3_body(dims, a3, z3, w3, l3, i4, i3, g3):
+def back3_body(dims, t3, z3, w3, i4, i3, g3):
     H, L, HB, C1, C2, C3, C4, C5 = dims
     band = lax.axis_index("rows")
     own, ph = (HB // 4, PH // 4)
-    taps(3, a3, z3, g3, l3, band, HB, H, spread_up(i4, 0), ROWS3 - 2, 2, 4)
+    pre_grads(3, t3, z3, g3, band, HB, H, spread_up(i4, 0), ROWS3 - 2, 2, own + 4)
     n = own + 2
     lhs = three(lambda dr, dc: g3[dr : dr + n, dc : dc + ph].reshape(n * ph * L, C3))
     rhs = jnp.concatenate([w3[t * C2 : (t + 1) * C2, :] for t in range(8, -1, -1)], axis=1)
     i3[...] = (dot_t(lhs, rhs) * 0.25).reshape(n, ph, L, C2)
 
 
-def back2_body(dims, a2, z2, w2t, l2, i3, i2, g2):
+def back2_body(dims, t2, z2, w2t, i3, i2, g2):
     H, L, HB, C1, C2, C3, C4, C5 = dims
     band = lax.axis_index("rows")
     own, ph = (HB // 2, PH // 4)
-    taps(2, a2, z2, g2, l2, band, HB, H, spread_up(i3, 1), ROWS2 - 2, 2, 4)
+    pre_grads(2, t2, z2, g2, band, HB, H, spread_up(i3, 1), ROWS2 - 2, 2, 6)
     step = (own + 2) // 2
     for r0 in (0, step):
         lhs = jnp.concatenate(
@@ -531,7 +542,7 @@
             i2[r0 : r0 + step, u] = out[..., u * LANES : (u + 1) * LANES]
 
 
-def back1_body(dims, a1, z1, r1, l1, i2, grad_ref, g1):
+def back1_body(dims, t1, z1, r1, i2, grad_ref, g1):
     H, L, HB, C1, C2, C3, C4, C5 = dims
     band = lax.axis_index("rows")
     ph = PH // 4
@@ -541,12 +552,15 @@
         v = jnp.stack([v[:, q % 2, q // 2] for q in range(2 * ph)], axis=1)
         return jnp.stack([v[(j + 1) // 2] for j in range(chunk)])
 
-    taps(1, a1, z1, g1, l1, band, HB, H, up, ROWS1 - 1, 1, 6)
+    pre_grads(1, t1, z1, g1, band, HB, H, up, ROWS1 - 1, 1, 6)
     lhs = jnp.concatenate(
-        [g1[dr : dr + HB, j].reshape(HB * L, LANES) for dr in range(3) for j in range(PH // 2 + 2)],
-        axis=1,
+        [g1[:, j].reshape((HB + 2) * L, LANES) for j in range(PH // 2 + 2)], axis=1
     )
-    gin = dot_t(lhs, r1[...])
+    rows3 = dot_t(lhs, r1[...]).reshape(HB + 2, L, 2 * LANES)
+    first = rows3[0:HB, :, 0:LANES].reshape(HB * L, LANES)
+    second = rows3[1 : HB + 1, :, 0:LANES].reshape(HB * L, LANES)
+    third = rows3[2 : HB + 2, :, LANES : 2 * LANES].reshape(HB * L, LANES)
+    gin = (first + pltpu.roll(second, HALF, 1) + third)[:, 0:HALF]
     high = gin.astype(BF16)
     split = jnp.concatenate([high.astype(F32), gin - high.astype(F32)], axis=1).astype(BF16)
     width = PH * L
@@ -560,11 +574,13 @@
         grad_ref[ch] = jnp.sum(wide.reshape(HB, L, width), axis=1)
 
 
-ROWS1, ROWS2, ROWS3, ROWS4 = (8, 4, 4, 4)
+ROWS1, ROWS2, ROWS3, ROWS4 = (8, 4, 4, 8)
+TAP_ROWS = (6, 4, 4, 0, 0)
 
 
 def frame_work(x, c1, c2, b1, convs, biases, linears, HB):
-    H, L, _ = x.shape
+    H, L, _ = x[0].shape
+    H = H * len(x)
     C1, C2, C3, C4, C5 = [c.shape[-1] for c in convs]
     dims = (H, L, HB, C1, C2, C3, C4, C5)
     ph2, ph3, ph4 = (PH // 2, PH // 4, PH // 8)
@@ -575,7 +591,7 @@
         weights_body,
         (
             V((4 * HALF, PH * HALF), BF16),
-            V((HALF, 3 * (ph2 + 2) * LANES), BF16),
+            V((4 * HALF, (ph2 + 2) * LANES), BF16),
             V((12 * C1, 2 * C2), BF16),
             V((4 * C1, 12 * C2), BF16),
         ),
@@ -592,25 +608,28 @@
         (H // 16 + 4, 1, L, C5),
     )
     outs = (V((8, LANES), F32),)
-    outs += tuple(V((2,) + s, BF16) for s in acts) + tuple(V(s, F32) for s in acts)
+    halos = (1, 2, 2, 2, 2)
+    outs += tuple(V(((HB >> i) + 2 * halos[i],) + s[1:], F32) for i, s in enumerate(acts))
+    outs += tuple(V(s, F32) for s in acts)
     outs += tuple(V(v.shape, v.dtype) for v in far)
-    loss, a1, a2, a3, a4, a5, z1, z2, z3, z4, z5, w3, w4, w5, *vecs = call(
+    loss, t1, t2, t3, t4, t5, z1, z2, z3, z4, z5, w3, w4, w5, *_ = call(
         functools.partial(forward_body, dims),
         outs,
-        (x, w1, w2),
+        (*x, w1, w2),
         "forward",
         (
+            V((H + 2, L, LANES), BF16),
             V((2, H, L, 2 * LANES), BF16),
             V((2, H // 2 + 2, ph2, L, LANES), BF16),
             V((2, H // 4 + 2, ph3 + 2, L, C2), BF16),
             V((2, H // 8 + 2, ph4 + 2, L, C3), BF16),
             V((2, H // 16 + 2, 3, L, C4), BF16),
+            *[V((2,) + s, BF16) for s in acts],
             pltpu.SemaphoreType.DMA((12,)),
         ),
-        limit=24,
+        limit=32,
         far=far,
     )
-    l = vecs[4:]
     n1, n2, n3, n4, n5 = (HB + 2, HB // 2 + 4, HB // 4 + 4, HB // 8 + 4, HB // 16 + 4)
 
     def step(body, name, ins, out, scratch, flops):
@@ -618,30 +637,30 @@
 
     def back5(_):
         return step(
-            back5_body, "back5", (a5, z5, w5, l[4]), V((n5 - 2, 1, L, C4), F32), (n5, 3, L, C5), FL
+            back5_body, "back5", (t5, z5, w5), V((n5 - 2, 1, L, C4), F32), (n5, 3, L, C5), FL
         )
 
     def back4(i5):
         return step(
-            back4_body, "back4", (a4, z4, w4, l[3], i5), V((n4 - 2, ph4, L, C3), F32),
+            back4_body, "back4", (t4, z4, w4, i5), V((n4 - 2, ph4, L, C3), F32),
             (n4, ph4 + 2, L, C4), FL,
         )
 
     def back3(i4):
         return step(
-            back3_body, "back3", (a3, z3, w3, l[2], i4), V((n3 - 2, ph3, L, C2), F32),
+            back3_body, "back3", (t3, z3, w3, i4), V((n3 - 2, ph3, L, C2), F32),
             (n3, ph3 + 2, L, C3), FL,
         )
 
     def back2(i3):
         return step(
-            back2_body, "back2", (a2, z2, w2t, l[1], i3), V((n2 - 2, 2, ph3, L, LANES), F32),
+            back2_body, "back2", (t2, z2, w2t, i3), V((n2 - 2, 2, ph3, L, LANES), F32),
             (n2, 2, ph3 + 2, L, C2), FL,
         )
 
     def back1(i2):
         return step(
-            back1_body, "back1", (a1, z1, r1, l[0], i2),
+            back1_body, "back1", (t1, z1, r1, i2),
             jax.ShapeDtypeStruct((3, HB, L * PH), F32), (n1, ph2 + 2, L, LANES), FL,
         )
 
@@ -649,6 +668,28 @@
 
 
 FL = 10**9
+
+
+def sum_stages(size):
+    bits = [1 << k for k in range(size.bit_length() - 1)]
+    assert size == 1 << len(bits)
+    stages = [bits[:1]]
+    for k in range(1, len(bits), 2):
+        pair = bits[k : k + 2]
+        stages.append(pair + [pair[0] ^ pair[1]] if len(pair) == 2 else pair)
+    return stages
+
+
+def gather_bands(x):
+    size = lax.axis_size("rows")
+    assert size & (size - 1) == 0
+    blocks = {0: x}
+    hops = [h for h in (1 << k for k in range(size.bit_length() - 1))][::-1]
+    for hop in hops:
+        pairs = [(i, i ^ hop) for i in range(size)]
+        for m in list(blocks):
+            blocks[m ^ hop] = lax.ppermute(blocks[m], "rows", pairs)
+    return [blocks[m] for m in range(size)]
 
 
 def on_device(real_frames, fake_frames, *params):
@@ -661,26 +702,22 @@
         c1, c2, b1 = (convs[0], convs[1], biases[0].reshape(1, -1))
         c2 = c2.reshape(9, *c2.shape[2:])
         x, c1, c2, b1 = prep(real_frames[n], fake_frames[n], c1, c2, b1)
-        x = lax.all_gather(x, "rows", axis=0, tiled=True)
+        x = gather_bands(x)
         work.append(frame_work(x, c1, c2, b1, convs, biases, linears, band_rows))
     total = functools.reduce(jnp.add, [loss for loss, _ in work])
-    hops = []
-    for axis in ("rows", "dp"):
-        hop = 1
-        while hop < lax.axis_size(axis):
-            hops.append((axis, hop))
-            hop *= 2
+    axes = ("dp", "rows")
+    size = lax.axis_size(axes)
+    stages = sum_stages(size)
     states = [None] * frames
-    for stage in range(max(5, len(hops))):
-        if stage < len(hops):
-            axis, hop = hops[stage]
-            pairs = [(i, i ^ hop) for i in range(lax.axis_size(axis))]
-            other = lax.ppermute(total, axis, pairs)
-        if stage < 5:
-            states = [steps[stage](s) for s, (_, steps) in zip(states, work)]
-        if stage < len(hops):
-            total, other, states = lax.optimization_barrier((total, other, states))
-            total = total + other
+    done = 0
+    for stage, hops in enumerate(stages):
+        others = [lax.ppermute(total, axes, [(i, i ^ hop) for i in range(size)]) for hop in hops]
+        last = 5 if stage == len(stages) - 1 else min(5, 1 + 2 * stage)
+        for k in range(done, last):
+            states = [steps[k](s) for s, (_, steps) in zip(states, work)]
+        done = last
+        total, others, states = lax.optimization_barrier((total, others, states))
+        total = functools.reduce(jnp.add, others, total)
     counts = [frame_total * (band_rows * bands >> s) * (width >> s) for s in range(5)]
     losses = jnp.sum(total, axis=1)[0:5] * jnp.array([1.0 / c for c in counts], F32)
     return (losses, jnp.stack(states))

time: 46.5 us -> 39.5 us (0.85)
  Pallas kernels: 29.4 us -> 21.6 us
  blocking collectives: 7.22 us -> 0 us
  waiting for transfers between devices: 0.46 us -> 5.03 us
  starting transfers between devices: 7.81 us -> 11.3 us
    pallas_call x8, Pallas kernels: 29.4 us -> 21.6 us  [call(): pl.pallas_call(body, out_shape=outs, in_specs=[HBM] * len(far) + [VM] * l...]
    all_gather x1 -> x0, blocking collectives: 7.22 us -> none  [on_device(): x = lax.all_gather(x, 'rows', axis=0, tiled=True)]
    ppermute x5 -> x10, waiting for transfers between devices: 0.46 us -> 5.03 us  [the longest x3 3.13 us: gather_bands(): blocks[m ^ hop] = lax.ppermute(blocks[m], 'rows', pairs)]
    ppermute x5 -> x10, starting transfers between devices: 7.81 us -> 11.3 us  [the longest x7 8.31 us: on_device(): lax.ppermute(total, axes, [(i, i ^ hop) for i in range(size)])]
  transfers between devices with their start and end apart: 5 -> 10, of which waited for: 1 -> 5; matrix products, arithmetic and copies ran while one was open for 0% -> 0% of each run, Pallas kernels for 25% -> 18%
where the time goes in v1:
time: 39.5 us; the launch traced here: 39.3 us
  Pallas kernels  21.6 us (55%)
  starting transfers between devices  11.3 us (29%)
  waiting for transfers between devices  5.03 us (13%)
  between operations  0.73 us (2%)
  other arithmetic  0.64 us (2%)
    pallas_call x8, Pallas kernels, call(): pl.pallas_call(body, out_shape=outs, in_specs=[HBM] * len(far) + [VM] * l...  21.6 us
    ppermute x7, starting transfers between devices, on_device(): lax.ppermute(total, axes, [(i, i ^ hop) for i in range(size)])  8.31 us
    ppermute x3, waiting for transfers between devices, gather_bands(): blocks[m ^ hop] = lax.ppermute(blocks[m], 'rows', pairs)  3.13 us
    ppermute x3, starting transfers between devices, gather_bands(): blocks[m ^ hop] = lax.ppermute(blocks[m], 'rows', pairs)  3.04 us
    ppermute x7, waiting for transfers between devices, on_device(): lax.ppermute(total, axes, [(i, i ^ hop) for i in range(size)])  1.9 us
  transfers between devices with their start and end apart: 10, of which 5 were waited for; matrix products, arithmetic and copies ran while one was open for 0% of the time, Pallas kernels for 18%

profile of v1, /device:TPU:0, one launch (start us, length us, event | category | flops | bytes accessed | tf_op | source)
XLA Modules:
  0.0 39.3 jit_solution(11385066071765482519)
XLA Ops:
  0.6 1.6 %prep.1 = (bf16[16,16,128]{2,1,0:T(8,128)(2,1)S(1)}, bf16[3,3,3,64]{3,2,1,0:T(4,128)(2,1)S(1)}, bf16[9,64,128]{2,1,0:T(8,128)(2,1)S(1)}, f32[1,64]{1,0:T(1,128)S(1)}) custom-call(bf16[3,16,256]{2,1,0:T(8,128)(2,1)} %bitcast.22, bf16[3,16,256]{2,1,0:T(8,128)(2,1)} %bitcast.23, bf16[3,3,3,64]{3,2,1,0:T(4,128)(2,1)} %c1_hbm.1, bf16[9,64,128]{2,1,0:T(8,128)(2,1)} %bitcast.20, ...), custom_call_target="tpu_custom_call" | custom-call | tf_op jit(solution)/shard_map/prep/pallas_call | solution.py:65
  2.2 3.0 %collective-permute-start.1 = (bf16[16,16,128]{2,1,0:T(8,128)(2,1)S(1)}, bf16[16,16,128]{2,1,0:T(8,128)(2,1)S(1)}, u32[]{:S(2)}, u32[]{:S(2)}) collective-permute-start(bf16[16,16,128]{2,1,0:T(8,128)(2,1)S(1)} %get-tuple-element.37.refs_12_), channel_id=1, source_target_pairs={{0,2},{1,3},{2,0},{3,1},{4,6},{5,7},{6,4},{7,5},{8,10},{9,11},{10,... | collective-permute-start | bytes 196616 | tf_op jit(solution)/shard_map/ppermute | solution.py:691
  5.3 2.2 %collective-permute-done.1.refs_14_ = bf16[16,16,128]{2,1,0:T(8,128)(2,1)S(1)} collective-permute-done((bf16[16,16,128]{2,1,0:T(8,128)(2,1)S(1)}, bf16[16,16,128]{2,1,0:T(8,128)(2,1)S(1)}, u32[]{:S(2)}, u32[]{:S(2)}) %collective-permute-start.1) | collective-permute-done | bytes 65568 | tf_op jit(solution)/shard_map/ppermute | solution.py:691
  7.5 0.0 collective-permute-start.2
  7.5 0.3 weights.1
  7.9 0.9 %collective-permute-done.2.refs_15_ = bf16[16,16,128]{2,1,0:T(8,128)(2,1)S(1)} collective-permute-done((bf16[16,16,128]{2,1,0:T(8,128)(2,1)S(1)}, bf16[16,16,128]{2,1,0:T(8,128)(2,1)S(1)}, u32[]{:S(2)}, u32[]{:S(2)}) %collective-permute-start.2) | collective-permute-done | bytes 65568 | tf_op jit(solution)/shard_map/ppermute | solution.py:691
  8.8 12.9 %forward.1 = (f32[8,128]{1,0:T(8,128)S(1)}, f32[18,8,16,128]{3,2,1,0:T(8,128)S(1)}, f32[12,2,4,16,128]{4,3,2,1,0:T(8,128)S(1)}, f32[8,4,16,256]{3,2,1,0:T(8,128)...) custom-call(bf16[1152,256]{1,0:T(8,128)(2,1)} %bitcast.19, ...), custom_call_target="tpu_custom_call" | custom-call | tf_op jit(solution)/shard_map/forward/pallas_call | solution.py:65
  21.7 0.2 collective-permute-start.3
  21.9 1.5 %back5.1.i5 = f32[3,1,16,512]{3,2,1,0:T(8,128)S(1)} custom-call(f32[5,1,16,512]{3,2,1,0:T(8,128)S(1)} %get-tuple-element.44.t5, f32[8,1,16,512]{3,2,1,0:T(8,128)S(1)} %get-tuple-element.45.z5, bf16[4608,512]{1,0:T(8,128)(2,1)S(1)} %get-tuple-element.46.w5), custom_call_target="tpu_custom_call" | custom-call | flops 1000000000 | tf_op jit(solution)/shard_map/back5/pallas_call | solution.py:65
  23.4 3.0 %collective-permute-start.6 = (f32[8,128]{1,0:T(8,128)S(1)}, f32[8,128]{1,0:T(8,128)S(1)}, u32[]{:S(2)}, u32[]{:S(2)}) collective-permute-start(f32[8,128]{1,0:T(8,128)S(1)} %add.21), channel_id=1, source_target_pairs={{0,6},{1,7},{2,4},{3,5},{4,2},{5,3},{6,0},{7,1},{8,14},{9,15},{10,... | collective-permute-start | bytes 12296 | tf_op jit(solution)/shard_map/ppermute | solution.py:714
  26.5 0.5 %collective-permute-start.5 = (f32[8,128]{1,0:T(8,128)S(1)}, f32[8,128]{1,0:T(8,128)S(1)}, u32[]{:S(2)}, u32[]{:S(2)}) collective-permute-start(f32[8,128]{1,0:T(8,128)S(1)} %add.21), channel_id=1, source_target_pairs={{0,4},{1,5},{2,6},{3,7},{4,0},{5,1},{6,2},{7,3},{8,12},{9,13},{10,... | collective-permute-start | bytes 12296 | tf_op jit(solution)/shard_map/ppermute | solution.py:714
  27.0 0.1 collective-permute-start.4
  27.1 1.0 %back4.1.i4 = f32[4,2,16,256]{3,2,1,0:T(8,128)S(1)} custom-call(f32[6,2,16,512]{3,2,1,0:T(8,128)S(1)} %get-tuple-element.52.t4, f32[12,2,16,512]{3,2,1,0:T(8,128)S(1)} %get-tuple-element.53.z4, bf16[2304,512]{1,0:T(8,128)(2,1)S(1)} %get-tuple-element.54.w4, f32[3,1,16,512]{3,2,1,0:T(8,128)S(1)} %back5.1.i5), custom_call_target="tpu_custom_call" | custom-call | flops 1000000000 | tf_op jit(solution)/shard_map/back4/pallas_call | solution.py:65
  28.1 0.8 %back3.1.i3 = f32[6,4,16,128]{3,2,1,0:T(8,128)S(1)} custom-call(f32[8,4,16,256]{3,2,1,0:T(8,128)S(1)} %get-tuple-element.49.t3, f32[16,4,16,256]{3,2,1,0:T(8,128)S(1)} %get-tuple-element.50.z3, bf16[1152,256]{1,0:T(8,128)(2,1)S(1)} %get-tuple-element.51.w3, f32[4,2,16,256]{3,2,1,0:T(8,128)S(1)} %back4.1.i4), custom_call_target="tpu_custom_call" | custom-call | flops 1000000000 | tf_op jit(solution)/shard_map/back3/pallas_call | solution.py:65
  28.9 1.2 %collective-permute-done.5 = f32[8,128]{1,0:T(8,128)S(1)} collective-permute-done((f32[8,128]{1,0:T(8,128)S(1)}, f32[8,128]{1,0:T(8,128)S(1)}, u32[]{:S(2)}, u32[]{:S(2)}) %collective-permute-start.5) | collective-permute-done | bytes 4128 | tf_op jit(solution)/shard_map/ppermute | solution.py:714
  30.1 0.5 %collective-permute-done.4 = f32[8,128]{1,0:T(8,128)S(1)} collective-permute-done((f32[8,128]{1,0:T(8,128)S(1)}, f32[8,128]{1,0:T(8,128)S(1)}, u32[]{:S(2)}, u32[]{:S(2)}) %collective-permute-start.4) | collective-permute-done | bytes 4128 | tf_op jit(solution)/shard_map/ppermute | solution.py:714
  30.6 3.6 %collective-permute-start.9 = (f32[8,128]{1,0:T(8,128)S(1)}, f32[8,128]{1,0:T(8,128)S(1)}, u32[]{:S(2)}, u32[]{:S(2)}) collective-permute-start(f32[8,128]{1,0:T(8,128)S(1)} %add_add_fusion), channel_id=1, source_target_pairs={{0,24},{1,25},{2,26},{3,27},{4,28},{5,29},{6,30},{7,31},{8,16},{9,... | collective-permute-start | bytes 12296 | tf_op jit(solution)/shard_map/ppermute | solution.py:714
  34.2 0.8 %collective-permute-start.7 = (f32[8,128]{1,0:T(8,128)S(1)}, f32[8,128]{1,0:T(8,128)S(1)}, u32[]{:S(2)}, u32[]{:S(2)}) collective-permute-start(f32[8,128]{1,0:T(8,128)S(1)} %add_add_fusion), channel_id=1, source_target_pairs={{0,8},{1,9},{2,10},{3,11},{4,12},{5,13},{6,14},{7,15},{8,0},{9,1},... | collective-permute-start | bytes 12296 | tf_op jit(solution)/shard_map/ppermute | solution.py:714
  35.0 1.2 %back2.1.i2 = f32[10,2,4,16,128]{4,3,2,1,0:T(8,128)S(1)} custom-call(f32[12,2,4,16,128]{4,3,2,1,0:T(8,128)S(1)} %get-tuple-element.63.t2, f32[20,2,4,16,128]{4,3,2,1,0:T(8,128)S(1)} %get-tuple-element.64.z2, bf16[256,1536]{1,0:T(8,128)(2,1)S(1)} %get-tuple-element.65.w2t, f32[6,4,16,128]{3,2,1,0:T(8,128)S(1)} %back3.1.i3), custom_call_target="tpu_custom_call" | custom-call | flops 1000000000 | tf_op jit(solution)/shard_map/back2/pallas_call | solution.py:65
  36.1 0.0 copy-start
  36.2 2.3 %back1.1 = f32[3,16,256]{2,1,0:T(8,128)} custom-call(f32[18,8,16,128]{3,2,1,0:T(8,128)S(1)} %get-tuple-element.60.t1, f32[40,8,16,128]{3,2,1,0:T(8,128)S(1)} %get-tuple-element.61.z1, bf16[256,1280]{1,0:T(8,128)(2,1)S(1)} %get-tuple-element.62.r1, f32[10,2,4,16,128]{4,3,2,1,0:T(8,128)S(1)} %back2.1.i2), custom_call_target="tpu_custom_call" | custom-call | flops 1000000000 | tf_op jit(solution)/shard_map/back1/pallas_call | solution.py:65
  38.5 0.2 collective-permute-done.8
  38.7 0.1 add_reduce_fusion
  38.8 0.5 %slice_multiply_fusion = f32[5]{0:T(128)} fusion(f32[5]{0:T(128)S(1)} %copy-done, f32[8]{0:T(128)S(1)} %add_reduce_fusion), kind=kLoop, calls=%fused_computation.2 | loop fusion | flops 5 | bytes 60 | tf_op jit(solution)/shard_map/mul | solution.py:722
  (10 shorter events, 0.0 us)
Async XLA Ops:
  2.2 5.3 %collective-permute-start.1 = (bf16[16,16,128]{2,1,0:T(8,128)(2,1)S(1)}, bf16[16,16,128]{2,1,0:T(8,128)(2,1)S(1)}, u32[]{:S(2)}, u32[]{:S(2)}) collective-permute-start(bf16[16,16,128]{2,1,0:T(8,128)(2,1)S(1)} %get-tuple-element.37.refs_12_), channel_id=1, source_target_pairs={{0,2},{1,3},{2,0},{3,1},{4,6},{5,7},{6,4},{7,5},{8,10},{9,11},{10,... | collective-permute-start | bytes 196616 | tf_op jit(solution)/shard_map/ppermute | solution.py:691
  5.3 2.6 %collective-permute-start = (bf16[16,16,128]{2,1,0:T(8,128)(2,1)S(1)}, bf16[16,16,128]{2,1,0:T(8,128)(2,1)S(1)}, u32[]{:S(2)}, u32[]{:S(2)}) collective-permute-start(bf16[16,16,128]{2,1,0:T(8,128)(2,1)S(1)} %get-tuple-element.37.refs_12_), channel_id=1, source_target_pairs={{0,1},{1,0},{2,3},{3,2},{4,5},{5,4},{6,7},{7,6},{8,9},{9,8},{10,11... | collective-permute-start | bytes 196616 | tf_op jit(solution)/shard_map/ppermute | solution.py:691
  7.5 1.3 %collective-permute-start.2 = (bf16[16,16,128]{2,1,0:T(8,128)(2,1)S(1)}, bf16[16,16,128]{2,1,0:T(8,128)(2,1)S(1)}, u32[]{:S(2)}, u32[]{:S(2)}) collective-permute-start(bf16[16,16,128]{2,1,0:T(8,128)(2,1)S(1)} %collective-permute-done.1.refs_14_), channel_id=1, source_target_pairs={{0,1},{1,0},{2,3},{3,2},{4,5},{5,4},{6,7},{7,6},{8,9},{9,8},{10,11... | collective-permute-start | bytes 196616 | tf_op jit(solution)/shard_map/ppermute | solution.py:691
  21.7 1.7 %collective-permute-start.3 = (f32[8,128]{1,0:T(8,128)S(1)}, f32[8,128]{1,0:T(8,128)S(1)}, u32[]{:S(2)}, u32[]{:S(2)}) collective-permute-start(f32[8,128]{1,0:T(8,128)S(1)} %get-tuple-element.47), channel_id=1, source_target_pairs={{0,1},{1,0},{2,3},{3,2},{4,5},{5,4},{6,7},{7,6},{8,9},{9,8},{10,11... | collective-permute-start | bytes 12296 | tf_op jit(solution)/shard_map/ppermute | solution.py:714
  23.4 5.5 %collective-permute-start.6 = (f32[8,128]{1,0:T(8,128)S(1)}, f32[8,128]{1,0:T(8,128)S(1)}, u32[]{:S(2)}, u32[]{:S(2)}) collective-permute-start(f32[8,128]{1,0:T(8,128)S(1)} %add.21), channel_id=1, source_target_pairs={{0,6},{1,7},{2,4},{3,5},{4,2},{5,3},{6,0},{7,1},{8,14},{9,15},{10,... | collective-permute-start | bytes 12296 | tf_op jit(solution)/shard_map/ppermute | solution.py:714
  26.5 3.6 %collective-permute-start.5 = (f32[8,128]{1,0:T(8,128)S(1)}, f32[8,128]{1,0:T(8,128)S(1)}, u32[]{:S(2)}, u32[]{:S(2)}) collective-permute-start(f32[8,128]{1,0:T(8,128)S(1)} %add.21), channel_id=1, source_target_pairs={{0,4},{1,5},{2,6},{3,7},{4,0},{5,1},{6,2},{7,3},{8,12},{9,13},{10,... | collective-permute-start | bytes 12296 | tf_op jit(solution)/shard_map/ppermute | solution.py:714
  27.0 3.6 %collective-permute-start.4 = (f32[8,128]{1,0:T(8,128)S(1)}, f32[8,128]{1,0:T(8,128)S(1)}, u32[]{:S(2)}, u32[]{:S(2)}) collective-permute-start(f32[8,128]{1,0:T(8,128)S(1)} %add.21), channel_id=1, source_target_pairs={{0,2},{1,3},{2,0},{3,1},{4,6},{5,7},{6,4},{7,5},{8,10},{9,11},{10,... | collective-permute-start | bytes 12296 | tf_op jit(solution)/shard_map/ppermute | solution.py:714
  30.6 7.9 %collective-permute-start.9 = (f32[8,128]{1,0:T(8,128)S(1)}, f32[8,128]{1,0:T(8,128)S(1)}, u32[]{:S(2)}, u32[]{:S(2)}) collective-permute-start(f32[8,128]{1,0:T(8,128)S(1)} %add_add_fusion), channel_id=1, source_target_pairs={{0,24},{1,25},{2,26},{3,27},{4,28},{5,29},{6,30},{7,31},{8,16},{9,... | collective-permute-start | bytes 12296 | tf_op jit(solution)/shard_map/ppermute | solution.py:714
  34.2 4.5 %collective-permute-start.8 = (f32[8,128]{1,0:T(8,128)S(1)}, f32[8,128]{1,0:T(8,128)S(1)}, u32[]{:S(2)}, u32[]{:S(2)}) collective-permute-start(f32[8,128]{1,0:T(8,128)S(1)} %add_add_fusion), channel_id=1, source_target_pairs={{0,16},{1,17},{2,18},{3,19},{4,20},{5,21},{6,22},{7,23},{8,24},{9,... | collective-permute-start | bytes 12296 | tf_op jit(solution)/shard_map/ppermute | solution.py:714
  34.2 4.5 %collective-permute-start.7 = (f32[8,128]{1,0:T(8,128)S(1)}, f32[8,128]{1,0:T(8,128)S(1)}, u32[]{:S(2)}, u32[]{:S(2)}) collective-permute-start(f32[8,128]{1,0:T(8,128)S(1)} %add_add_fusion), channel_id=1, source_target_pairs={{0,8},{1,9},{2,10},{3,11},{4,12},{5,13},{6,14},{7,15},{8,0},{9,1},... | collective-permute-start | bytes 12296 | tf_op jit(solution)/shard_map/ppermute | solution.py:714
  36.1 2.6 %copy-start = (f32[5]{0:T(128)S(1)}, f32[5]{0:T(128)}, u32[]{:S(2)}) copy-start(f32[5]{0:T(128)} %constant.4.clone) | copy-start | bytes 64

commit v2 on v1

--- a/solution.py
+++ b/solution.py
@@ -195,7 +195,7 @@
 
 
 def inverse_norms(r, f, ones2, chans):
-    sums = dot(jnp.concatenate([r * r, f * f], axis=1).astype(BF16), ones2)
+    sums = dot(jnp.concatenate([r * r, f * f], axis=1), ones2)
     reps = chans // LANES
 
     def spread(v):
@@ -266,7 +266,7 @@
                 for i in range(2):
                     lanes = slice(i * LANES, (i + 1) * LANES)
                     part = act[:, lanes].reshape(rows, L, LANES)
-                    a1[img, kept, n * 2 + i] = part.astype(BF16)
+                    a1[img, pl.ds(r0 + PAD, rows), n * 2 + i] = part.astype(BF16)
                     if img:
                         z1[kept, n * 2 + i] = h[:, lanes].reshape(rows, L, LANES)
                     pair = part.reshape(rows // 2, 2, L, LANES)
@@ -288,12 +288,11 @@
 
     rows2, rows3, rows4 = (ROWS2, ROWS3, ROWS4)
     loss_ref[...] = jnp.zeros(loss_ref.shape, F32)
-    places = (rows - 1, rows2 - 2, rows3 - 2, band * (HB // 8), band * (HB // 16))
 
     def tap(seg):
         s = seg - 1
         acts = (a1, a2, a3, a4, a5)[s]
-        taps(seg, acts, (t1, t2, t3, t4, t5)[s], l_refs[s], loss_ref, HB >> s, places[s])
+        taps(seg, acts, (t1, t2, t3, t4, t5)[s], l_refs[s], loss_ref, HB >> s, band, H // HB)
 
     for copy in copies[:3]:
         copy.wait()
@@ -318,7 +317,7 @@
             act = gelu(h)
             for u in range(2):
                 lanes = slice(u * C2, (u + 1) * C2)
-                a2[img, kept, u] = act[:, lanes].astype(BF16).reshape(rows2, ph3, L, C2)
+                a2[img, pl.ds(r0 + PAD, rows2), u] = act[:, lanes].astype(BF16).reshape(rows2, ph3, L, C2)
                 if img:
                     z2[kept, u] = h[:, lanes].reshape(rows2, ph3, L, C2)
             s = (act[:, 0:C2] + act[:, C2 : 2 * C2]).reshape(rows2 // 2, 2, ph3, L, C2)
@@ -338,7 +337,7 @@
             )
             h = dot(lhs, w3[...]) + bias3
             act = gelu(h)
-            a3[img, kept] = act.astype(BF16).reshape(rows3, ph3, L, C3)
+            a3[img, pl.ds(r0 + PAD, rows3)] = act.astype(BF16).reshape(rows3, ph3, L, C3)
             if img:
                 z3[kept] = h.reshape(rows3, ph3, L, C3)
             pair = act.reshape(rows3 // 2, 2, ph4, 2, L, C3)
@@ -397,12 +396,13 @@
     tap(5)
 
 
-def taps(seg, acts, grads, l_ref, loss_ref, own, local):
+def taps(seg, acts, grads, l_ref, loss_ref, own, band, bands):
     chans = acts.shape[-1]
     inner = acts.shape[2:-1]
     halo = 1 if seg == 1 else 2
     count = own + 2 * halo
     chunk = TAP_ROWS[seg - 1] or count
+    local = band * own - halo + PAD
     m = chunk * math.prod(inner)
     scale = -2.0 * 4.0 ** (seg - 1)
     ones2 = ones_for(seg, chans)
@@ -415,28 +415,44 @@
     def piece(k):
         i0 = k * chunk
         at = pl.ds(local + i0, chunk)
-        r = acts[0, at].reshape(m, chans).astype(F32)
-        f = acts[1, at].reshape(m, chans).astype(F32)
+        r = acts[0, at].reshape(m, chans)
+        f = acts[1, at].reshape(m, chans)
         inv_r, inv_f = inverse_norms(r, f, ones2, chans)
-        nf = f * inv_f
-        d = r * inv_r - nf
+        nf = f.astype(F32) * inv_f
+        d = r.astype(F32) * inv_r - nf
         ld = lin * d
         q = dot((nf * ld).astype(BF16), ones1)
         if reps > 1:
             q = jnp.concatenate([q] * reps, axis=1)
         tap = (ld - nf * q) * (inv_f * scale)
         grads[pl.ds(i0, chunk)] = tap.reshape((chunk,) + inner + (chans,))
-        mapped = (ld * d).reshape((chunk,) + inner + (chans,))
+        mapped = (d * d).reshape((chunk,) + inner + (chans,))
         place = iota(mapped.shape, 0) + i0
         mapped = jnp.where((place >= halo) & (place < halo + own), mapped, 0.0)
-        part = jnp.sum(mapped.reshape(m, chans), axis=0, keepdims=True)
+        add(mapped)
+
+    def add(mapped):
+        part = jnp.sum(mapped.reshape(-1, chans), axis=0, keepdims=True) * lin
         acc = part[:, 0:LANES]
         for j in range(1, reps):
             acc = acc + part[:, j * LANES : (j + 1) * LANES]
         loss_ref[seg - 1 : seg, :] += acc
 
+    def other(row, size):
+        at = pl.ds(row, size)
+        m = size * math.prod(inner)
+        r = acts[0, at].reshape(m, chans)
+        f = acts[1, at].reshape(m, chans)
+        inv_r, inv_f = inverse_norms(r, f, ones2, chans)
+        d = r.astype(F32) * inv_r - f.astype(F32) * inv_f
+        add(d * d)
+
     for k in range(count // chunk):
         piece(k)
+    size = min(own, OTHER_ROWS[seg - 1])
+    for m_ in range(2, bands, 2):
+        for k in range(own // size):
+            other((band ^ m_) * own + PAD + k * size, size)
 
 
 def pre_grads(seg, tap_ref, pres, grads, band, HB, H, up, local, halo, chunk):
@@ -576,6 +592,8 @@
 
 ROWS1, ROWS2, ROWS3, ROWS4 = (8, 4, 4, 8)
 TAP_ROWS = (6, 4, 4, 0, 0)
+OTHER_ROWS = (4, 4, 4, 2, 1)
+PAD = 2
 
 
 def frame_work(x, c1, c2, b1, convs, biases, linears, HB):
@@ -624,7 +642,7 @@
             V((2, H // 4 + 2, ph3 + 2, L, C2), BF16),
             V((2, H // 8 + 2, ph4 + 2, L, C3), BF16),
             V((2, H // 16 + 2, 3, L, C4), BF16),
-            *[V((2,) + s, BF16) for s in acts],
+            *[V((2, (H >> i) + 2 * PAD) + s[1:], BF16) for i, s in enumerate(acts)],
             pltpu.SemaphoreType.DMA((12,)),
         ),
         limit=32,
@@ -668,16 +686,6 @@
 
 
 FL = 10**9
-
-
-def sum_stages(size):
-    bits = [1 << k for k in range(size.bit_length() - 1)]
-    assert size == 1 << len(bits)
-    stages = [bits[:1]]
-    for k in range(1, len(bits), 2):
-        pair = bits[k : k + 2]
-        stages.append(pair + [pair[0] ^ pair[1]] if len(pair) == 2 else pair)
-    return stages
 
 
 def gather_bands(x):
@@ -705,19 +713,21 @@
         x = gather_bands(x)
         work.append(frame_work(x, c1, c2, b1, convs, biases, linears, band_rows))
     total = functools.reduce(jnp.add, [loss for loss, _ in work])
-    axes = ("dp", "rows")
-    size = lax.axis_size(axes)
-    stages = sum_stages(size)
+    hops = [("rows", 1)]
+    size = lax.axis_size("dp")
+    hops += [("dp", 1 << k) for k in range(size.bit_length() - 1)]
+    assert size == 1 << len(hops) - 1
     states = [None] * frames
     done = 0
-    for stage, hops in enumerate(stages):
-        others = [lax.ppermute(total, axes, [(i, i ^ hop) for i in range(size)]) for hop in hops]
-        last = 5 if stage == len(stages) - 1 else min(5, 1 + 2 * stage)
+    for stage, (axis, hop) in enumerate(hops):
+        pairs = [(i, i ^ hop) for i in range(lax.axis_size(axis))]
+        other = lax.ppermute(total, axis, pairs)
+        last = 5 if stage == len(hops) - 1 else (1, 3, 4)[min(stage, 2)]
         for k in range(done, last):
             states = [steps[k](s) for s, (_, steps) in zip(states, work)]
         done = last
-        total, others, states = lax.optimization_barrier((total, others, states))
-        total = functools.reduce(jnp.add, others, total)
+        total, other, states = lax.optimization_barrier((total, other, states))
+        total = total + other
     counts = [frame_total * (band_rows * bands >> s) * (width >> s) for s in range(5)]
     losses = jnp.sum(total, axis=1)[0:5] * jnp.array([1.0 / c for c in counts], F32)
     return (losses, jnp.stack(states))

time: 39.5 us -> 38.2 us (0.967)
  waiting for transfers between devices: 5.03 us -> 3.73 us
  starting transfers between devices: 11.3 us -> 10.1 us
  Pallas kernels: 21.6 us -> 22.8 us
    ppermute x7 -> x4, waiting for transfers between devices: 1.9 us -> 0.6 us  [on_device(): other = lax.ppermute(total, axis, pairs)]
    ppermute x7 -> x4, starting transfers between devices: 8.31 us -> 7.06 us  [on_device(): other = lax.ppermute(total, axis, pairs)]
    pallas_call x8, Pallas kernels: 21.6 us -> 22.8 us  [call(): pl.pallas_call(body, out_shape=outs, in_specs=[HBM] * len(far) + [VM] * l...]
  transfers between devices with their start and end apart: 10 -> 7, of which waited for: 5 -> 3; matrix products, arithmetic and copies ran while one was open for 0% -> 0% of each run, Pallas kernels for 18% -> 19%
where the time goes in v2:
time: 38.2 us; the launch traced here: 38 us
  Pallas kernels  22.8 us (60%)
  starting transfers between devices  10.1 us (26%)
  waiting for transfers between devices  3.73 us (10%)
  between operations  0.73 us (2%)
  other arithmetic  0.64 us (2%)
    pallas_call x8, Pallas kernels, call(): pl.pallas_call(body, out_shape=outs, in_specs=[HBM] * len(far) + [VM] * l...  22.8 us
    ppermute x4, starting transfers between devices, on_device(): other = lax.ppermute(total, axis, pairs)  7.06 us
    ppermute x3, waiting for transfers between devices, gather_bands(): blocks[m ^ hop] = lax.ppermute(blocks[m], 'rows', pairs)  3.13 us
    ppermute x3, starting transfers between devices, gather_bands(): blocks[m ^ hop] = lax.ppermute(blocks[m], 'rows', pairs)  3.04 us
  transfers between devices with their start and end apart: 7, of which 3 were waited for; matrix products, arithmetic and copies ran while one was open for 0% of the time, Pallas kernels for 19%

profile of v2, /device:TPU:0, one launch (start us, length us, event | category | flops | bytes accessed | tf_op | source)
XLA Modules:
  0.0 38.0 jit_solution(8526208455360992352)
XLA Ops:
  0.6 1.6 %prep.1 = (bf16[16,16,128]{2,1,0:T(8,128)(2,1)S(1)}, bf16[3,3,3,64]{3,2,1,0:T(4,128)(2,1)S(1)}, bf16[9,64,128]{2,1,0:T(8,128)(2,1)S(1)}, f32[1,64]{1,0:T(1,128)S(1)}) custom-call(bf16[3,16,256]{2,1,0:T(8,128)(2,1)} %bitcast.22, bf16[3,16,256]{2,1,0:T(8,128)(2,1)} %bitcast.23, bf16[3,3,3,64]{3,2,1,0:T(4,128)(2,1)} %c1_hbm.1, bf16[9,64,128]{2,1,0:T(8,128)(2,1)} %bitcast.20, ...), custom_call_target="tpu_custom_call" | custom-call | tf_op jit(solution)/shard_map/prep/pallas_call | solution.py:65
  2.2 3.0 %collective-permute-start.1 = (bf16[16,16,128]{2,1,0:T(8,128)(2,1)S(1)}, bf16[16,16,128]{2,1,0:T(8,128)(2,1)S(1)}, u32[]{:S(2)}, u32[]{:S(2)}) collective-permute-start(bf16[16,16,128]{2,1,0:T(8,128)(2,1)S(1)} %get-tuple-element.36.refs_12_), channel_id=1, source_target_pairs={{0,2},{1,3},{2,0},{3,1},{4,6},{5,7},{6,4},{7,5},{8,10},{9,11},{10,... | collective-permute-start | bytes 196616 | tf_op jit(solution)/shard_map/ppermute | solution.py:699
  5.3 0.0 collective-permute-start
  5.3 2.2 %collective-permute-done.1.refs_14_ = bf16[16,16,128]{2,1,0:T(8,128)(2,1)S(1)} collective-permute-done((bf16[16,16,128]{2,1,0:T(8,128)(2,1)S(1)}, bf16[16,16,128]{2,1,0:T(8,128)(2,1)S(1)}, u32[]{:S(2)}, u32[]{:S(2)}) %collective-permute-start.1) | collective-permute-done | bytes 65568 | tf_op jit(solution)/shard_map/ppermute | solution.py:699
  7.5 0.0 collective-permute-start.2
  7.5 0.3 weights.1
  7.9 0.0 collective-permute-done.refs_13_
  7.9 0.9 %collective-permute-done.2.refs_15_ = bf16[16,16,128]{2,1,0:T(8,128)(2,1)S(1)} collective-permute-done((bf16[16,16,128]{2,1,0:T(8,128)(2,1)S(1)}, bf16[16,16,128]{2,1,0:T(8,128)(2,1)S(1)}, u32[]{:S(2)}, u32[]{:S(2)}) %collective-permute-start.2) | collective-permute-done | bytes 65568 | tf_op jit(solution)/shard_map/ppermute | solution.py:699
  8.8 14.1 %forward.1 = (f32[8,128]{1,0:T(8,128)S(1)}, f32[18,8,16,128]{3,2,1,0:T(8,128)S(1)}, f32[12,2,4,16,128]{4,3,2,1,0:T(8,128)S(1)}, f32[8,4,16,256]{3,2,1,0:T(8,128)...) custom-call(bf16[1152,256]{1,0:T(8,128)(2,1)} %bitcast.19, ...), custom_call_target="tpu_custom_call" | custom-call | tf_op jit(solution)/shard_map/forward/pallas_call | solution.py:65
  22.9 0.2 collective-permute-start.3
  23.1 1.5 %back5.1.i5 = f32[3,1,16,512]{3,2,1,0:T(8,128)S(1)} custom-call(f32[5,1,16,512]{3,2,1,0:T(8,128)S(1)} %get-tuple-element.43.t5, f32[8,1,16,512]{3,2,1,0:T(8,128)S(1)} %get-tuple-element.44.z5, bf16[4608,512]{1,0:T(8,128)(2,1)S(1)} %get-tuple-element.45.w5), custom_call_target="tpu_custom_call" | custom-call | flops 1000000000 | tf_op jit(solution)/shard_map/back5/pallas_call | solution.py:65
  24.6 0.0 collective-permute-done.3
  24.7 2.1 %collective-permute-start.4 = (f32[8,128]{1,0:T(8,128)S(1)}, f32[8,128]{1,0:T(8,128)S(1)}, u32[]{:S(2)}, u32[]{:S(2)}) collective-permute-start(f32[8,128]{1,0:T(8,128)S(1)} %add.12), channel_id=1, source_target_pairs={{0,4},{4,0},{8,12},{12,8},{16,20},{20,16},{24,28},{28,24},{1,5},{5... | collective-permute-start | bytes 12296 | tf_op jit(solution)/shard_map/ppermute | solution.py:724
  26.8 1.0 %back4.1.i4 = f32[4,2,16,256]{3,2,1,0:T(8,128)S(1)} custom-call(f32[6,2,16,512]{3,2,1,0:T(8,128)S(1)} %get-tuple-element.51.t4, f32[12,2,16,512]{3,2,1,0:T(8,128)S(1)} %get-tuple-element.52.z4, bf16[2304,512]{1,0:T(8,128)(2,1)S(1)} %get-tuple-element.53.w4, f32[3,1,16,512]{3,2,1,0:T(8,128)S(1)} %back5.1.i5), custom_call_target="tpu_custom_call" | custom-call | flops 1000000000 | tf_op jit(solution)/shard_map/back4/pallas_call | solution.py:65
  27.7 0.8 %back3.1.i3 = f32[6,4,16,128]{3,2,1,0:T(8,128)S(1)} custom-call(f32[8,4,16,256]{3,2,1,0:T(8,128)S(1)} %get-tuple-element.48.t3, f32[16,4,16,256]{3,2,1,0:T(8,128)S(1)} %get-tuple-element.49.z3, bf16[1152,256]{1,0:T(8,128)(2,1)S(1)} %get-tuple-element.50.w3, f32[4,2,16,256]{3,2,1,0:T(8,128)S(1)} %back4.1.i4), custom_call_target="tpu_custom_call" | custom-call | flops 1000000000 | tf_op jit(solution)/shard_map/back3/pallas_call | solution.py:65
  28.5 0.0 collective-permute-done.4
  28.6 1.9 %collective-permute-start.5 = (f32[8,128]{1,0:T(8,128)S(1)}, f32[8,128]{1,0:T(8,128)S(1)}, u32[]{:S(2)}, u32[]{:S(2)}) collective-permute-start(f32[8,128]{1,0:T(8,128)S(1)} %add.13), channel_id=1, source_target_pairs={{0,8},{4,12},{8,0},{12,4},{16,24},{20,28},{24,16},{28,20},{1,9},{5... | collective-permute-start | bytes 12296 | tf_op jit(solution)/shard_map/ppermute | solution.py:724
  30.4 1.2 %back2.1.i2 = f32[10,2,4,16,128]{4,3,2,1,0:T(8,128)S(1)} custom-call(f32[12,2,4,16,128]{4,3,2,1,0:T(8,128)S(1)} %get-tuple-element.57.t2, f32[20,2,4,16,128]{4,3,2,1,0:T(8,128)S(1)} %get-tuple-element.58.z2, bf16[256,1536]{1,0:T(8,128)(2,1)S(1)} %get-tuple-element.59.w2t, f32[6,4,16,128]{3,2,1,0:T(8,128)S(1)} %back3.1.i3), custom_call_target="tpu_custom_call" | custom-call | flops 1000000000 | tf_op jit(solution)/shard_map/back2/pallas_call | solution.py:65
  31.6 0.6 %collective-permute-done.5 = f32[8,128]{1,0:T(8,128)S(1)} collective-permute-done((f32[8,128]{1,0:T(8,128)S(1)}, f32[8,128]{1,0:T(8,128)S(1)}, u32[]{:S(2)}, u32[]{:S(2)}) %collective-permute-start.5) | collective-permute-done | bytes 4128 | tf_op jit(solution)/shard_map/ppermute | solution.py:724
  32.2 2.8 %collective-permute-start.6 = (f32[8,128]{1,0:T(8,128)S(1)}, f32[8,128]{1,0:T(8,128)S(1)}, u32[]{:S(2)}, u32[]{:S(2)}) collective-permute-start(f32[8,128]{1,0:T(8,128)S(1)} %add.14), channel_id=1, source_target_pairs={{0,16},{4,20},{8,24},{12,28},{16,0},{20,4},{24,8},{28,12},{1,17},{... | collective-permute-start | bytes 12296 | tf_op jit(solution)/shard_map/ppermute | solution.py:724
  35.1 2.3 %back1.1 = f32[3,16,256]{2,1,0:T(8,128)} custom-call(f32[18,8,16,128]{3,2,1,0:T(8,128)S(1)} %get-tuple-element.63.t1, f32[40,8,16,128]{3,2,1,0:T(8,128)S(1)} %get-tuple-element.64.z1, bf16[256,1280]{1,0:T(8,128)(2,1)S(1)} %get-tuple-element.65.r1, f32[10,2,4,16,128]{4,3,2,1,0:T(8,128)S(1)} %back2.1.i2), custom_call_target="tpu_custom_call" | custom-call | flops 1000000000 | tf_op jit(solution)/shard_map/back1/pallas_call | solution.py:65
  37.4 0.0 collective-permute-done.6
  37.4 0.1 add_reduce_fusion
  37.5 0.5 %slice_multiply_fusion = f32[5]{0:T(128)} fusion(f32[5]{0:T(128)S(1)} %copy-done, f32[8]{0:T(128)S(1)} %add_reduce_fusion), kind=kLoop, calls=%fused_computation.1 | loop fusion | flops 5 | bytes 60 | tf_op jit(solution)/shard_map/mul | solution.py:732
  (5 shorter events, 0.0 us)
Async XLA Ops:
  2.2 5.3 %collective-permute-start.1 = (bf16[16,16,128]{2,1,0:T(8,128)(2,1)S(1)}, bf16[16,16,128]{2,1,0:T(8,128)(2,1)S(1)}, u32[]{:S(2)}, u32[]{:S(2)}) collective-permute-start(bf16[16,16,128]{2,1,0:T(8,128)(2,1)S(1)} %get-tuple-element.36.refs_12_), channel_id=1, source_target_pairs={{0,2},{1,3},{2,0},{3,1},{4,6},{5,7},{6,4},{7,5},{8,10},{9,11},{10,... | collective-permute-start | bytes 196616 | tf_op jit(solution)/shard_map/ppermute | solution.py:699
  5.3 2.6 %collective-permute-start = (bf16[16,16,128]{2,1,0:T(8,128)(2,1)S(1)}, bf16[16,16,128]{2,1,0:T(8,128)(2,1)S(1)}, u32[]{:S(2)}, u32[]{:S(2)}) collective-permute-start(bf16[16,16,128]{2,1,0:T(8,128)(2,1)S(1)} %get-tuple-element.36.refs_12_), channel_id=1, source_target_pairs={{0,1},{1,0},{2,3},{3,2},{4,5},{5,4},{6,7},{7,6},{8,9},{9,8},{10,11... | collective-permute-start | bytes 196616 | tf_op jit(solution)/shard_map/ppermute | solution.py:699
  7.5 1.3 %collective-permute-start.2 = (bf16[16,16,128]{2,1,0:T(8,128)(2,1)S(1)}, bf16[16,16,128]{2,1,0:T(8,128)(2,1)S(1)}, u32[]{:S(2)}, u32[]{:S(2)}) collective-permute-start(bf16[16,16,128]{2,1,0:T(8,128)(2,1)S(1)} %collective-permute-done.1.refs_14_), channel_id=1, source_target_pairs={{0,1},{1,0},{2,3},{3,2},{4,5},{5,4},{6,7},{7,6},{8,9},{9,8},{10,11... | collective-permute-start | bytes 196616 | tf_op jit(solution)/shard_map/ppermute | solution.py:699
  22.9 1.7 %collective-permute-start.3 = (f32[8,128]{1,0:T(8,128)S(1)}, f32[8,128]{1,0:T(8,128)S(1)}, u32[]{:S(2)}, u32[]{:S(2)}) collective-permute-start(f32[8,128]{1,0:T(8,128)S(1)} %get-tuple-element.46), channel_id=1, source_target_pairs={{0,1},{1,0},{2,3},{3,2},{4,5},{5,4},{6,7},{7,6},{8,9},{9,8},{10,11... | collective-permute-start | bytes 12296 | tf_op jit(solution)/shard_map/ppermute | solution.py:724
  24.7 3.9 %collective-permute-start.4 = (f32[8,128]{1,0:T(8,128)S(1)}, f32[8,128]{1,0:T(8,128)S(1)}, u32[]{:S(2)}, u32[]{:S(2)}) collective-permute-start(f32[8,128]{1,0:T(8,128)S(1)} %add.12), channel_id=1, source_target_pairs={{0,4},{4,0},{8,12},{12,8},{16,20},{20,16},{24,28},{28,24},{1,5},{5... | collective-permute-start | bytes 12296 | tf_op jit(solution)/shard_map/ppermute | solution.py:724
  28.6 3.7 %collective-permute-start.5 = (f32[8,128]{1,0:T(8,128)S(1)}, f32[8,128]{1,0:T(8,128)S(1)}, u32[]{:S(2)}, u32[]{:S(2)}) collective-permute-start(f32[8,128]{1,0:T(8,128)S(1)} %add.13), channel_id=1, source_target_pairs={{0,8},{4,12},{8,0},{12,4},{16,24},{20,28},{24,16},{28,20},{1,9},{5... | collective-permute-start | bytes 12296 | tf_op jit(solution)/shard_map/ppermute | solution.py:724
  32.2 5.1 %collective-permute-start.6 = (f32[8,128]{1,0:T(8,128)S(1)}, f32[8,128]{1,0:T(8,128)S(1)}, u32[]{:S(2)}, u32[]{:S(2)}) collective-permute-start(f32[8,128]{1,0:T(8,128)S(1)} %add.14), channel_id=1, source_target_pairs={{0,16},{4,20},{8,24},{12,28},{16,0},{20,4},{24,8},{28,12},{1,17},{... | collective-permute-start | bytes 12296 | tf_op jit(solution)/shard_map/ppermute | solution.py:724
  35.1 2.4 %copy-start = (f32[5]{0:T(128)S(1)}, f32[5]{0:T(128)}, u32[]{:S(2)}) copy-start(f32[5]{0:T(128)} %constant.4.clone) | copy-start | bytes 64

commit v3 on v2

--- a/solution.py
+++ b/solution.py
@@ -253,7 +253,7 @@
 
     rows = ROWS1
 
-    @pl.loop(0, H // rows, unroll=2)
+    @pl.loop(0, H // rows, unroll=4)
     def _(step):
         r0 = step * rows
         kept = keep(r0, rows, HB + 2 * rows, band * HB - rows)

time: 38.2 us -> 38.2 us (level)
  no operation moved by 1% of the time
where the time goes in v3:
time: 38.2 us; the launch traced here: 38 us
  Pallas kernels  22.8 us (60%)
  starting transfers between devices  10.1 us (26%)
  waiting for transfers between devices  3.74 us (10%)
  between operations  0.73 us (2%)
  other arithmetic  0.64 us (2%)
    pallas_call x8, Pallas kernels, call(): pl.pallas_call(body, out_shape=outs, in_specs=[HBM] * len(far) + [VM] * l...  22.8 us
    ppermute x4, starting transfers between devices, on_device(): other = lax.ppermute(total, axis, pairs)  7.04 us
    ppermute x3, waiting for transfers between devices, gather_bands(): blocks[m ^ hop] = lax.ppermute(blocks[m], 'rows', pairs)  3.13 us
    ppermute x3, starting transfers between devices, gather_bands(): blocks[m ^ hop] = lax.ppermute(blocks[m], 'rows', pairs)  3.04 us
  transfers between devices with their start and end apart: 7, of which 3 were waited for; matrix products, arithmetic and copies ran while one was open for 0% of the time, Pallas kernels for 19%

profile of v3, /device:TPU:0, one launch (start us, length us, event | category | flops | bytes accessed | tf_op | source)
XLA Modules:
  0.0 38.0 jit_solution(10231632202615131247)
XLA Ops:
  0.6 1.6 %prep.1 = (bf16[16,16,128]{2,1,0:T(8,128)(2,1)S(1)}, bf16[3,3,3,64]{3,2,1,0:T(4,128)(2,1)S(1)}, bf16[9,64,128]{2,1,0:T(8,128)(2,1)S(1)}, f32[1,64]{1,0:T(1,128)S(1)}) custom-call(bf16[3,16,256]{2,1,0:T(8,128)(2,1)} %bitcast.22, bf16[3,16,256]{2,1,0:T(8,128)(2,1)} %bitcast.23, bf16[3,3,3,64]{3,2,1,0:T(4,128)(2,1)} %c1_hbm.1, bf16[9,64,128]{2,1,0:T(8,128)(2,1)} %bitcast.20, ...), custom_call_target="tpu_custom_call" | custom-call | tf_op jit(solution)/shard_map/prep/pallas_call | solution.py:65
  2.2 3.0 %collective-permute-start.1 = (bf16[16,16,128]{2,1,0:T(8,128)(2,1)S(1)}, bf16[16,16,128]{2,1,0:T(8,128)(2,1)S(1)}, u32[]{:S(2)}, u32[]{:S(2)}) collective-permute-start(bf16[16,16,128]{2,1,0:T(8,128)(2,1)S(1)} %get-tuple-element.36.refs_12_), channel_id=1, source_target_pairs={{0,2},{1,3},{2,0},{3,1},{4,6},{5,7},{6,4},{7,5},{8,10},{9,11},{10,... | collective-permute-start | bytes 196616 | tf_op jit(solution)/shard_map/ppermute | solution.py:699
  5.3 0.0 collective-permute-start
  5.3 2.2 %collective-permute-done.1.refs_14_ = bf16[16,16,128]{2,1,0:T(8,128)(2,1)S(1)} collective-permute-done((bf16[16,16,128]{2,1,0:T(8,128)(2,1)S(1)}, bf16[16,16,128]{2,1,0:T(8,128)(2,1)S(1)}, u32[]{:S(2)}, u32[]{:S(2)}) %collective-permute-start.1) | collective-permute-done | bytes 65568 | tf_op jit(solution)/shard_map/ppermute | solution.py:699
  7.5 0.0 collective-permute-start.2
  7.5 0.3 weights.1
  7.9 0.0 collective-permute-done.refs_13_
  7.9 0.9 %collective-permute-done.2.refs_15_ = bf16[16,16,128]{2,1,0:T(8,128)(2,1)S(1)} collective-permute-done((bf16[16,16,128]{2,1,0:T(8,128)(2,1)S(1)}, bf16[16,16,128]{2,1,0:T(8,128)(2,1)S(1)}, u32[]{:S(2)}, u32[]{:S(2)}) %collective-permute-start.2) | collective-permute-done | bytes 65568 | tf_op jit(solution)/shard_map/ppermute | solution.py:699
  8.8 14.2 %forward.1 = (f32[8,128]{1,0:T(8,128)S(1)}, f32[18,8,16,128]{3,2,1,0:T(8,128)S(1)}, f32[12,2,4,16,128]{4,3,2,1,0:T(8,128)S(1)}, f32[8,4,16,256]{3,2,1,0:T(8,128)...) custom-call(bf16[1152,256]{1,0:T(8,128)(2,1)} %bitcast.19, ...), custom_call_target="tpu_custom_call" | custom-call | tf_op jit(solution)/shard_map/forward/pallas_call | solution.py:65
  22.9 0.2 collective-permute-start.3
  23.2 1.5 %back5.1.i5 = f32[3,1,16,512]{3,2,1,0:T(8,128)S(1)} custom-call(f32[5,1,16,512]{3,2,1,0:T(8,128)S(1)} %get-tuple-element.43.t5, f32[8,1,16,512]{3,2,1,0:T(8,128)S(1)} %get-tuple-element.44.z5, bf16[4608,512]{1,0:T(8,128)(2,1)S(1)} %get-tuple-element.45.w5), custom_call_target="tpu_custom_call" | custom-call | flops 1000000000 | tf_op jit(solution)/shard_map/back5/pallas_call | solution.py:65
  24.7 0.0 collective-permute-done.3
  24.7 2.1 %collective-permute-start.4 = (f32[8,128]{1,0:T(8,128)S(1)}, f32[8,128]{1,0:T(8,128)S(1)}, u32[]{:S(2)}, u32[]{:S(2)}) collective-permute-start(f32[8,128]{1,0:T(8,128)S(1)} %add.12), channel_id=1, source_target_pairs={{0,4},{4,0},{8,12},{12,8},{16,20},{20,16},{24,28},{28,24},{1,5},{5... | collective-permute-start | bytes 12296 | tf_op jit(solution)/shard_map/ppermute | solution.py:724
  26.8 1.0 %back4.1.i4 = f32[4,2,16,256]{3,2,1,0:T(8,128)S(1)} custom-call(f32[6,2,16,512]{3,2,1,0:T(8,128)S(1)} %get-tuple-element.51.t4, f32[12,2,16,512]{3,2,1,0:T(8,128)S(1)} %get-tuple-element.52.z4, bf16[2304,512]{1,0:T(8,128)(2,1)S(1)} %get-tuple-element.53.w4, f32[3,1,16,512]{3,2,1,0:T(8,128)S(1)} %back5.1.i5), custom_call_target="tpu_custom_call" | custom-call | flops 1000000000 | tf_op jit(solution)/shard_map/back4/pallas_call | solution.py:65
  27.8 0.8 %back3.1.i3 = f32[6,4,16,128]{3,2,1,0:T(8,128)S(1)} custom-call(f32[8,4,16,256]{3,2,1,0:T(8,128)S(1)} %get-tuple-element.48.t3, f32[16,4,16,256]{3,2,1,0:T(8,128)S(1)} %get-tuple-element.49.z3, bf16[1152,256]{1,0:T(8,128)(2,1)S(1)} %get-tuple-element.50.w3, f32[4,2,16,256]{3,2,1,0:T(8,128)S(1)} %back4.1.i4), custom_call_target="tpu_custom_call" | custom-call | flops 1000000000 | tf_op jit(solution)/shard_map/back3/pallas_call | solution.py:65
  28.6 0.0 collective-permute-done.4
  28.6 1.9 %collective-permute-start.5 = (f32[8,128]{1,0:T(8,128)S(1)}, f32[8,128]{1,0:T(8,128)S(1)}, u32[]{:S(2)}, u32[]{:S(2)}) collective-permute-start(f32[8,128]{1,0:T(8,128)S(1)} %add.13), channel_id=1, source_target_pairs={{0,8},{4,12},{8,0},{12,4},{16,24},{20,28},{24,16},{28,20},{1,9},{5... | collective-permute-start | bytes 12296 | tf_op jit(solution)/shard_map/ppermute | solution.py:724
  30.5 1.2 %back2.1.i2 = f32[10,2,4,16,128]{4,3,2,1,0:T(8,128)S(1)} custom-call(f32[12,2,4,16,128]{4,3,2,1,0:T(8,128)S(1)} %get-tuple-element.57.t2, f32[20,2,4,16,128]{4,3,2,1,0:T(8,128)S(1)} %get-tuple-element.58.z2, bf16[256,1536]{1,0:T(8,128)(2,1)S(1)} %get-tuple-element.59.w2t, f32[6,4,16,128]{3,2,1,0:T(8,128)S(1)} %back3.1.i3), custom_call_target="tpu_custom_call" | custom-call | flops 1000000000 | tf_op jit(solution)/shard_map/back2/pallas_call | solution.py:65
  31.7 0.6 %collective-permute-done.5 = f32[8,128]{1,0:T(8,128)S(1)} collective-permute-done((f32[8,128]{1,0:T(8,128)S(1)}, f32[8,128]{1,0:T(8,128)S(1)}, u32[]{:S(2)}, u32[]{:S(2)}) %collective-permute-start.5) | collective-permute-done | bytes 4128 | tf_op jit(solution)/shard_map/ppermute | solution.py:724
  32.3 2.8 %collective-permute-start.6 = (f32[8,128]{1,0:T(8,128)S(1)}, f32[8,128]{1,0:T(8,128)S(1)}, u32[]{:S(2)}, u32[]{:S(2)}) collective-permute-start(f32[8,128]{1,0:T(8,128)S(1)} %add.14), channel_id=1, source_target_pairs={{0,16},{4,20},{8,24},{12,28},{16,0},{20,4},{24,8},{28,12},{1,17},{... | collective-permute-start | bytes 12296 | tf_op jit(solution)/shard_map/ppermute | solution.py:724
  35.1 2.3 %back1.1 = f32[3,16,256]{2,1,0:T(8,128)} custom-call(f32[18,8,16,128]{3,2,1,0:T(8,128)S(1)} %get-tuple-element.63.t1, f32[40,8,16,128]{3,2,1,0:T(8,128)S(1)} %get-tuple-element.64.z1, bf16[256,1280]{1,0:T(8,128)(2,1)S(1)} %get-tuple-element.65.r1, f32[10,2,4,16,128]{4,3,2,1,0:T(8,128)S(1)} %back2.1.i2), custom_call_target="tpu_custom_call" | custom-call | flops 1000000000 | tf_op jit(solution)/shard_map/back1/pallas_call | solution.py:65
  37.4 0.0 collective-permute-done.6
  37.4 0.1 add_reduce_fusion
  37.5 0.5 %slice_multiply_fusion = f32[5]{0:T(128)} fusion(f32[5]{0:T(128)S(1)} %copy-done, f32[8]{0:T(128)S(1)} %add_reduce_fusion), kind=kLoop, calls=%fused_computation.1 | loop fusion | flops 5 | bytes 60 | tf_op jit(solution)/shard_map/mul | solution.py:732
  (5 shorter events, 0.0 us)
Async XLA Ops:
  2.2 5.3 %collective-permute-start.1 = (bf16[16,16,128]{2,1,0:T(8,128)(2,1)S(1)}, bf16[16,16,128]{2,1,0:T(8,128)(2,1)S(1)}, u32[]{:S(2)}, u32[]{:S(2)}) collective-permute-start(bf16[16,16,128]{2,1,0:T(8,128)(2,1)S(1)} %get-tuple-element.36.refs_12_), channel_id=1, source_target_pairs={{0,2},{1,3},{2,0},{3,1},{4,6},{5,7},{6,4},{7,5},{8,10},{9,11},{10,... | collective-permute-start | bytes 196616 | tf_op jit(solution)/shard_map/ppermute | solution.py:699
  5.3 2.6 %collective-permute-start = (bf16[16,16,128]{2,1,0:T(8,128)(2,1)S(1)}, bf16[16,16,128]{2,1,0:T(8,128)(2,1)S(1)}, u32[]{:S(2)}, u32[]{:S(2)}) collective-permute-start(bf16[16,16,128]{2,1,0:T(8,128)(2,1)S(1)} %get-tuple-element.36.refs_12_), channel_id=1, source_target_pairs={{0,1},{1,0},{2,3},{3,2},{4,5},{5,4},{6,7},{7,6},{8,9},{9,8},{10,11... | collective-permute-start | bytes 196616 | tf_op jit(solution)/shard_map/ppermute | solution.py:699
  7.5 1.3 %collective-permute-start.2 = (bf16[16,16,128]{2,1,0:T(8,128)(2,1)S(1)}, bf16[16,16,128]{2,1,0:T(8,128)(2,1)S(1)}, u32[]{:S(2)}, u32[]{:S(2)}) collective-permute-start(bf16[16,16,128]{2,1,0:T(8,128)(2,1)S(1)} %collective-permute-done.1.refs_14_), channel_id=1, source_target_pairs={{0,1},{1,0},{2,3},{3,2},{4,5},{5,4},{6,7},{7,6},{8,9},{9,8},{10,11... | collective-permute-start | bytes 196616 | tf_op jit(solution)/shard_map/ppermute | solution.py:699
  22.9 1.7 %collective-permute-start.3 = (f32[8,128]{1,0:T(8,128)S(1)}, f32[8,128]{1,0:T(8,128)S(1)}, u32[]{:S(2)}, u32[]{:S(2)}) collective-permute-start(f32[8,128]{1,0:T(8,128)S(1)} %get-tuple-element.46), channel_id=1, source_target_pairs={{0,1},{1,0},{2,3},{3,2},{4,5},{5,4},{6,7},{7,6},{8,9},{9,8},{10,11... | collective-permute-start | bytes 12296 | tf_op jit(solution)/shard_map/ppermute | solution.py:724
  24.7 3.9 %collective-permute-start.4 = (f32[8,128]{1,0:T(8,128)S(1)}, f32[8,128]{1,0:T(8,128)S(1)}, u32[]{:S(2)}, u32[]{:S(2)}) collective-permute-start(f32[8,128]{1,0:T(8,128)S(1)} %add.12), channel_id=1, source_target_pairs={{0,4},{4,0},{8,12},{12,8},{16,20},{20,16},{24,28},{28,24},{1,5},{5... | collective-permute-start | bytes 12296 | tf_op jit(solution)/shard_map/ppermute | solution.py:724
  28.6 3.7 %collective-permute-start.5 = (f32[8,128]{1,0:T(8,128)S(1)}, f32[8,128]{1,0:T(8,128)S(1)}, u32[]{:S(2)}, u32[]{:S(2)}) collective-permute-start(f32[8,128]{1,0:T(8,128)S(1)} %add.13), channel_id=1, source_target_pairs={{0,8},{4,12},{8,0},{12,4},{16,24},{20,28},{24,16},{28,20},{1,9},{5... | collective-permute-start | bytes 12296 | tf_op jit(solution)/shard_map/ppermute | solution.py:724
  32.3 5.1 %collective-permute-start.6 = (f32[8,128]{1,0:T(8,128)S(1)}, f32[8,128]{1,0:T(8,128)S(1)}, u32[]{:S(2)}, u32[]{:S(2)}) collective-permute-start(f32[8,128]{1,0:T(8,128)S(1)} %add.14), channel_id=1, source_target_pairs={{0,16},{4,20},{8,24},{12,28},{16,0},{20,4},{24,8},{28,12},{1,17},{... | collective-permute-start | bytes 12296 | tf_op jit(solution)/shard_map/ppermute | solution.py:724
  35.1 2.4 %copy-start = (f32[5]{0:T(128)S(1)}, f32[5]{0:T(128)}, u32[]{:S(2)}) copy-start(f32[5]{0:T(128)} %constant.4.clone) | copy-start | bytes 64
